TPU v7x, 256 devices: a whole 4x4x8 slice. The times are simulated.
256 devices in a mesh: seq: 32 (over z_lo, x, core), res: 8 (over z_hi, y).
Axes of the slice: x: 4, y: 4, z: 8 (z_hi: 2, z_lo: 4; z = z_hi * 4 + z_lo), core: 2. Of those that a mesh axis runs over, the one named last changes fastest.
Arguments:
- embedded_aligned_rows: bfloat16 [96, 1024, 768], P('seq', 'res'), may hold values from -12 to 12
- norm_multiplier: float32 [768], replicated, may hold values from 0.1 to 1.9
- asker_projector: bfloat16 [768, 768], replicated, may hold values from -1 to 1
- matcher_projector: bfloat16 [768, 768], replicated, may hold values from -1 to 1
- content_projector: bfloat16 [768, 768], replicated, may hold values from -0.21875 to 0.21875
- final_projector: bfloat16 [768, 768], replicated, may hold values from -0.21875 to 0.21875
Outputs:
- mixed: bfloat16 [96, 1024, 768], P('seq', 'res')
All inputs are finite; a program needn't handle non-finite values.
Results may differ from a plain program's by a relative error of at most 0.01.
Values may be sent and summed in bfloat16 or wider, within the bound.
A program may use at most 64 MiB of HBM per device.

v0:
```python
import jax
import jax.numpy as jnp
from jax import lax
from jax.sharding import PartitionSpec as P

HEADS = 12


def side_by_side(arrays, axis, dim, along):
    widths = [a.shape[along] for a in arrays]
    both = jnp.concatenate(arrays, axis=along)
    out = lax.all_gather(both, axis, axis=dim, tiled=True)
    return tuple(jnp.split(out, [sum(widths[:k]) for k in range(1, len(widths))], axis=along))


def in_blocks(array, dim, count):
    before, after = (array.shape[:dim], array.shape[dim + 1 :])
    return jnp.moveaxis(array.reshape(*before, count, -1, *after), dim, 0)


def sent_and_summed(array, axis, dim):
    parts = in_blocks(array, dim, lax.axis_size(axis))
    arrived = lax.all_to_all(parts, axis, split_axis=0, concat_axis=0, tiled=True)
    return arrived.astype(jnp.float32).sum(axis=0)


def standardize_rows(embedded_aligned_rows, norm_multiplier):
    content_array = embedded_aligned_rows.astype(jnp.float32)
    center = content_array - jnp.mean(content_array, axis=-1, keepdims=True)
    spread = jnp.mean(center * center, axis=-1, keepdims=True)
    return (center / jnp.sqrt(spread + 1e-05) * norm_multiplier).astype(jnp.bfloat16)


def body(
    embedded_aligned_rows,
    norm_multiplier,
    asker_projector,
    matcher_projector,
    content_projector,
    final_projector,
):
    row_portion, column_portion, embedding_dimension = embedded_aligned_rows.shape
    heads = HEADS
    hsize = embedding_dimension // heads
    unrolled_array = standardize_rows(embedded_aligned_rows, norm_multiplier).reshape(
        row_portion * column_portion, embedding_dimension
    )
    query = jnp.dot(unrolled_array, asker_projector, preferred_element_type=jnp.float32).astype(
        jnp.bfloat16
    )
    query = query.reshape(row_portion, column_portion, heads, hsize)
    key_local = jnp.dot(
        unrolled_array, matcher_projector, preferred_element_type=jnp.float32
    ).astype(jnp.bfloat16)
    key_local = key_local.reshape(row_portion, column_portion, embedding_dimension)
    value_local = jnp.dot(
        unrolled_array, content_projector, preferred_element_type=jnp.float32
    ).astype(jnp.bfloat16)
    value_local = value_local.reshape(row_portion, column_portion, embedding_dimension)
    total_seqs = row_portion * lax.axis_size("seq")
    scale = 1.0 / (jnp.sqrt(jnp.float32(hsize)) * jnp.sqrt(jnp.float32(total_seqs)))
    key_all, value_all = side_by_side((key_local, value_local), "res", 1, 0)
    keys = key_all.reshape(row_portion, key_all.shape[1], heads, hsize)
    logits = jnp.einsum("sihe,sjhe->hij", query, keys, preferred_element_type=jnp.float32)
    share = sent_and_summed(logits.astype(jnp.bfloat16), "seq", 1)
    share_probs = jax.nn.softmax(share * scale, axis=-1).astype(jnp.bfloat16)
    probs = lax.all_gather(share_probs, "seq", axis=1, tiled=True)
    content_array = value_all.reshape(row_portion, value_all.shape[1], heads, hsize)
    attended = jnp.einsum(
        "hij,sjhe->sihe", probs, content_array, preferred_element_type=jnp.float32
    )
    attended = attended.astype(jnp.bfloat16).reshape(
        row_portion * column_portion, embedding_dimension
    )
    mixed = jnp.dot(attended, final_projector, preferred_element_type=jnp.float32).astype(
        jnp.bfloat16
    )
    return mixed.reshape(row_portion, column_portion, embedding_dimension)


def solution(mesh):
    placed = (P("seq", "res", None), P(), P(), P(), P(), P())
    return jax.shard_map(
        body, mesh=mesh, in_specs=placed, out_specs=P("seq", "res", None), check_vma=False
    )
```

profile of v0, /device:TPU:33, one launch (start us, length us, event | category | flops | bytes accessed | tf_op | source)
XLA Modules:
  0.0 389.0 jit_solution(7130635105588150745)
XLA Ops:
  6.5 0.0 copy-start
  6.5 0.0 copy-start.1
  6.5 0.0 copy-start.2
  6.5 0.0 all-gather.3.cloned.1.call-start
  6.5 1.4 convert_reduce_fusion.1
  7.9 1.4 fusion.20
  9.3 0.0 copy-done.1
  9.3 0.0 copy-done.2
  9.3 0.2 fusion.22
  9.6 0.0 copy-done
  9.6 0.0 copy-start.3
  9.6 0.6 convolution_convert_fusion.2
  10.2 0.6 copy-done.3
  10.8 0.6 convolution_convert_fusion.3
  11.5 0.3 copy.24
  11.8 0.3 copy.25
  12.1 1.1 pad_maximum_fusion
  13.2 0.0 copy-start.4
  13.2 0.0 all-gather.3.cloned.1.call-update
  13.2 0.0 all-gather.5.cloned.1.call-start
  13.3 1.2 copy-done.4
  14.5 0.6 convolution_convert_fusion.1
  15.1 1.0 reshape.53
  16.1 197.1 %all-gather.3.cloned.1.call-done = bf16[6,1024,768]{1,2,0:T(8,128)(2,1)} async-done(((bf16[6,128,768]{1,2,0:T(8,128)(2,1)}), bf16[6,1024,768]{1,2,0:T(8,128)(2,1)}) %all-gather.3.cloned.1.call-update) | async-done | bytes 9437200 | tf_op jit(solution)/shard_map/all_gather | solution.py:12
  213.2 7.2 %fusion.31 = (bf16[3,1024,768]{1,2,0:T(8,128)(2,1)}, bf16[3,1024,768]{1,2,0:T(8,128)(2,1)S(1)}) fusion(bf16[6,1024,768]{1,2,0:T(8,128)(2,1)} %all-gather.3.cloned.1.call-done), kind=kLoop, calls=%fused_computation.35 | loop fusion | bytes 18874368 | tf_op jit(solution)/shard_map/split | solution.py:13
  220.4 2.8 bitcast_convert_fusion
  223.2 5.7 %reshape.48 = bf16[12,32,4,1024]{3,2,1,0:T(4,128)(2,1)} reshape(bf16[12,128,1024]{2,1,0:T(8,128)(2,1)} %bitcast_convert_fusion) | data formatting | bytes 6291456 | tf_op jit(solution)/shard_map/reshape | solution.py:18
  229.0 3.6 copy.64
  232.5 79.5 %all_to_all.5 = bf16[32,12,4,1024]{3,2,1,0:T(4,128)(2,1)S(1)} all-to-all(bf16[32,12,4,1024]{3,2,1,0:T(4,128)(2,1)S(1)} %bitcast.29), channel_id=1, replica_groups=mesh['seq'=32,'res'=8] {'seq'}, dimensions={0} | all-to-all | bytes 6291456 | tf_op jit(solution)/shard_map/all_to_all | solution.py:23
  312.0 1.4 convert_reduce_fusion
  313.4 0.2 fusion.32
  313.7 0.1 divide_convert_fusion
  313.8 0.7 copy.30
  314.5 0.0 all-gather.5.cloned.1.call-update
  314.5 58.7 %all-gather.5.cloned.1.call-done = bf16[12,128,1024]{2,0,1:T(8,128)(2,1)} async-done(((bf16[12,4,1024]{2,0,1:T(8,128)(2,1)}), bf16[12,128,1024]{2,0,1:T(8,128)(2,1)}) %all-gather.5.cloned.1.call-update) | async-done | bytes 3145744 | tf_op jit(solution)/shard_map/all_gather | solution.py:67
  373.2 6.2 %fusion.15 = bf16[3,128,12,64]{1,3,0,2:T(8,128)(2,1)S(1)} fusion(bf16[12,128,1024,1]{2,0,1,3:T(8,128)(2,1)} %bitcast.38, bf16[3,1024,12,64]{1,3,2,0:T(8,128)(2,1)} %bitcast.30), kind=kOutput, calls=%fused_computation.18 | convolution fusion | flops 604274688 | bytes 8454144 | tf_op jit(solution)/shard_map/hij,sjhe->sihe/dot_general | solution.py:69
  379.4 0.0 copy-start.5
  379.4 0.5 copy.33
  380.0 0.7 copy-done.5
  380.7 1.5 convolution_convert_fusion
  (2 shorter events, 0.0 us)
Async XLA Ops:
  6.5 3.0 copy-start
  6.5 2.8 copy-start.1
  6.5 2.8 copy-start.2
  6.5 206.7 %all-gather.3.cloned.1.call-start = ((), (), s32[]{:S(2)}) async-start(), calls=%async_computation.1 | async-start | bytes 10616832 | tf_op jit(solution)/shard_map/all_gather | solution.py:12
  9.6 1.3 copy-start.3
  13.2 1.3 copy-start.4
  13.2 360.0 %all-gather.5.cloned.1.call-start = ((), (), s32[]{:S(2)}) async-start(), calls=%async_computation.2 | async-start | bytes 4325376 | tf_op jit(solution)/shard_map/all_gather | solution.py:67
  379.4 1.3 copy-start.5
Sparse Core Ops, SparseCore 0:
  13.4 199.8 all-gather.2
  314.6 58.5 all-gather.4
where the time goes:
time: 391 us; the launch traced here: 389 us
  waiting for transfers between devices  256 us (65%)
  blocking collectives  79.5 us (20%)
  local copies, waits for them, and re-layouts  21.8 us (6%)
  between operations  13.5 us (3%)
  matrix products  12.4 us (3%)
  other arithmetic  5.83 us (1%)
    all_gather x1, waiting for transfers between devices, side_by_side(): out = lax.all_gather(both, axis, axis=dim, tiled=True)  197 us
    all_to_all x1, blocking collectives, sent_and_summed(): lax.all_to_all(parts, axis, split_axis=0, concat_axis=0, tiled=True)  79.5 us
    all_gather x1, waiting for transfers between devices, body(): probs = lax.all_gather(share_probs, 'seq', axis=1, tiled=True)  58.7 us
    reshape x2, local copies, waits for them, and re-layouts, in_blocks(): return jnp.moveaxis(array.reshape(*before, count, -1, *after), dim, 0)  9.29 us
  transfers between devices with their start and end apart: 2, of which 2 were waited for; matrix products, arithmetic and copies ran while one was open for 0% of the time, Pallas kernels for 0%

commit v1 on v0

v1 whole, which is shorter than its diff:
```python
import functools

import jax
import jax.numpy as jnp
from jax import lax
from jax.experimental import pallas as pl
from jax.experimental.pallas import tpu as pltpu
from jax.sharding import PartitionSpec as P

MESH = pl.DeviceIdType.MESH
BF = jnp.bfloat16
F32 = jnp.float32
NX, NY, NZ = 4, 4, 4
S, B, D = 3, 128, 768
H, E = 3, 64
ROWS = 256
HALF = NY * B


def kernel(
    x_hbm, gain_ref, wq_hbm, wk_hbm, wv_hbm, wf_hbm, out_ref,
    xo, xp, xn, wq, wk, wv, wf, qt, kt, vt, qr, kr, vr, qn, xs, xr, zs, zr, pf, os, orr,
    lsem, zss, zrs, qss, qrs, kss, krs, vss, vrs, kfs, kfr, vfs, vfr,
    xss, xrs, lss, lrs, pzs, pzr, pxs, pxr, oss, osr,
):
    seq, res = lax.axis_index("seq"), lax.axis_index("res")
    c, x, zl = lax.rem(seq, 2), lax.rem(seq // 2, NX), seq // (2 * NX)
    y, zh = lax.rem(res, NY), res // NY

    def dev(x=x, zl=zl, c=c, y=y, zh=zh):
        return ((zl * NX + x) * 2 + c, zh * NY + y)

    def up(i, d, n):
        return lax.rem(i + d, n)

    other = dev(c=1 - c)

    def send(src, dst, ss, rs, to):
        return pltpu.make_async_remote_copy(
            src_ref=src, dst_ref=dst, send_sem=ss, recv_sem=rs, device_id=to, device_id_type=MESH
        )

    loads = [
        pltpu.make_async_copy(a, b, lsem.at[i])
        for i, (a, b) in enumerate(((x_hbm, xo), (wq_hbm, wq), (wk_hbm, wk), (wv_hbm, wv), (wf_hbm, wf)))
    ]
    for copy in loads:
        copy.start()

    barrier = pltpu.get_barrier_semaphore()
    peers = [other, dev(zh=1 - zh)]
    peers += [dev(x=up(x, d, NX)) for d in range(1, NX)]
    peers += [dev(zl=up(zl, d, NZ)) for d in range(1, NZ)]
    peers += [dev(y=up(y, d, NY), c=k) for d in range(1, NY) for k in range(2)]
    for peer in peers:
        pl.semaphore_signal(barrier, inc=1, device_id=peer, device_id_type=MESH)
    pl.semaphore_wait(barrier, len(peers))

    loads[0].wait()

    def rows_over(s):
        return send(xo.at[s], xp.at[s], zss.at[s], zrs.at[s], dev(zh=1 - zh))

    for s in range(S):
        rows_over(s).start()

    def norm(rows):
        rows = rows.astype(F32)
        center = rows - jnp.mean(rows, axis=-1, keepdims=True)
        spread = jnp.mean(center * center, axis=-1, keepdims=True)
        return (center * lax.rsqrt(spread + 1e-05) * gain_ref[...]).astype(BF)

    def project(normed, w):
        out = jnp.dot(normed, w[...], preferred_element_type=F32).astype(BF)
        return out.T.reshape(NY, H, E, B)

    def q_copy(s, d):
        b = (-d) % NY
        to = dev(y=up(y, d, NY), c=b // 2)
        return send(qt.at[up(y, d, NY), s], qr.at[b % 2, c, s], qss.at[d, s], qrs.at[b % 2, c, s], to)

    def kv_copy(t, r, ss, rs, half, s, d):
        g = up(y, d, NY)
        return send(
            t.at[half, g, s], r.at[half, (-d) % NY, c, s], ss.at[half, d - 1, s], rs.at[half, d - 1, s], dev(y=g)
        )

    def forward(r, ss, rs, half, rel):
        part = r.at[half, rel, c]
        return send(part, part, ss.at[half, rel], rs.at[half, rel], other)

    k_copy = functools.partial(kv_copy, kt, kr, kss, krs)
    v_copy = functools.partial(kv_copy, vt, vr, vss, vrs)
    k_forward = functools.partial(forward, kr, kfs, kfr)
    v_forward = functools.partial(forward, vr, vfs, vfr)

    for copy in loads[1:3]:
        copy.wait()

    @pl.loop(0, S)
    def _(s):
        normed = norm(xo[s])
        xn[s] = normed
        qt[:, s] = project(normed, wq)
        kt[0, :, s] = project(normed, wk)
        for d in range(1, NY):
            q_copy(s, d).start()

        @pl.when(c == 1)
        def _():
            q_copy(s, 0).start()

        @pl.when(c == 0)
        def _():
            qr[0, 0, s] = qt[y, s]

        for d in range(1, NY):
            k_copy(0, s, d).start()
        kr[0, 0, c, s] = kt[0, y, s]

    k_forward(0, 0).start()
    loads[3].wait()

    @pl.loop(0, S)
    def _(s):
        v = project(xn[s], wv)
        vt[0, :, s] = v
        vr[0, 0, c, s] = vt[0, y, s]

    v_forward(0, 0).start()

    def partner(s):
        rows_over(s).wait_recv()
        normed = norm(xp[s])
        kt[1, :, s] = project(normed, wk)
        for d in range(1, NY):
            k_copy(1, s, d).start()
        kr[1, 0, c, s] = kt[1, y, s]
        vt[1, :, s] = project(normed, wv)
        vr[1, 0, c, s] = vt[1, y, s]

    def forward_all(copy, fwd, half):
        for d in range(1, NY):
            for s in range(S):
                copy(half, s, d).wait_recv()
            fwd(half, (-d) % NY).start()

    def columns(r, half, h):
        return jnp.concatenate(
            [r[half, rel, :, :, h].reshape(2 * S * E, B) for rel in range(NY)], axis=1
        )

    def x_copy(half, d):
        g = up(x, d, NX)
        return send(xs.at[half, g], xr.at[half, d - 1], xss.at[half, d - 1], xrs.at[half, d - 1], dev(x=g))

    def z_copy(half, d):
        g = up(zl, d, NZ)
        return send(zs.at[half, g], zr.at[half, d - 1], lss.at[half, d - 1], lrs.at[half, d - 1], dev(zl=g))

    def logits(half):
        for rel in range(NY):
            k_forward(half, rel).wait_recv()

        @pl.loop(0, H)
        def _(h):
            part = jnp.dot(qn[h], columns(kr, half, h), preferred_element_type=F32).astype(BF)
            xs[half, :, h] = part.reshape(NX, ROWS // NX, HALF)

        for d in range(1, NX):
            x_copy(half, d).start()

    def over_x(half):
        for d in range(1, NX):
            x_copy(half, d).wait_recv()
        for h in range(H):
            total = xs[half, x, h].astype(F32)
            for d in range(1, NX):
                total += xr[half, d - 1, h].astype(F32)
            zs[half, :, h] = total.astype(BF).reshape(NZ, ROWS // NX // NZ, HALF)
        for d in range(1, NZ):
            z_copy(half, d).start()

    def over_z(half):
        for d in range(1, NZ):
            z_copy(half, d).wait_recv()
        total = zs[half, zl].astype(F32)
        for d in range(1, NZ):
            total += zr[half, d - 1].astype(F32)
        return total

    @pl.loop(0, 2)
    def _(s):
        partner(s)

    forward_all(k_copy, k_forward, 0)
    for b, k in ((0, 1), (1, 0), (1, 1)):
        for s in range(S):
            send(qt.at[0, s], qr.at[b, k, s], qss.at[0, s], qrs.at[b, k, s], other).wait_recv()

    @pl.when(c == 1)
    def _():
        for s in range(S):
            send(qt.at[0, s], qr.at[0, 0, s], qss.at[0, s], qrs.at[0, 0, s], other).wait_recv()

    @pl.loop(0, H)
    def _(h):
        cols = [qr[b, :, :, h].reshape(2 * S * E, B).T for b in range(2)]
        qn[h] = jnp.concatenate(cols, axis=0)

    logits(0)
    partner(2)
    k_forward(1, 0).start()
    v_forward(1, 0).start()

    @pl.loop(0, 2)
    def _(half):
        @pl.loop(0, S)
        def _(s):
            for d in range(1, NY):
                v_copy(half, s, d).start()

    over_x(0)
    forward_all(k_copy, k_forward, 1)
    logits(1)
    first = over_z(0)
    over_x(1)
    second = over_z(1)

    scale = 1.0 / (8.0 * (96.0 ** 0.5))
    top = jnp.maximum(jnp.max(first, axis=-1, keepdims=True), jnp.max(second, axis=-1, keepdims=True))
    first = jnp.exp((first - top) * scale)
    second = jnp.exp((second - top) * scale)
    whole = jnp.sum(first, axis=-1, keepdims=True) + jnp.sum(second, axis=-1, keepdims=True)
    inverse = 1.0 / whole
    pf[x, zl, :, :, :HALF] = (first * inverse).astype(BF)
    pf[x, zl, :, :, HALF:] = (second * inverse).astype(BF)

    def pz_copy(d):
        part = pf.at[x, zl]
        return send(part, part, pzs.at[d - 1], pzr.at[d - 1], dev(zl=up(zl, d, NZ)))

    def px_copy(d):
        part = pf.at[x]
        return send(part, part, pxs.at[d - 1], pxr.at[d - 1], dev(x=up(x, d, NX)))

    for d in range(1, NZ):
        pz_copy(d).start()
    for d in range(1, NZ):
        pz_copy(d).wait_recv()
    for d in range(1, NX):
        px_copy(d).start()
    for half in range(2):
        forward_all(v_copy, v_forward, half)
    for half in range(2):
        for rel in range(NY):
            v_forward(half, rel).wait_recv()
    for d in range(1, NX):
        px_copy(d).wait_recv()

    @pl.loop(0, H)
    def _(h):
        weights = pf[:, :, h].reshape(ROWS, 2 * HALF)
        total = jnp.zeros((2 * S * E, ROWS), F32)
        for half in range(2):
            total += lax.dot_general(
                columns(vr, half, h),
                weights[:, half * HALF : (half + 1) * HALF],
                (((1,), (1,)), ((), ())),
                preferred_element_type=F32,
            )
        total = total.astype(BF)
        for b in range(2):
            os[b, :, :, h] = total[:, b * B : (b + 1) * B].reshape(2, S, E, B)

    def o_copy(slot, k):
        b = 2 * c + slot
        return send(os.at[slot, k], orr.at[y], oss.at[slot, k], osr.at[b], dev(y=up(y, b, NY), c=k))

    for slot, k in ((1, 0), (1, 1), (0, 1)):
        o_copy(slot, k).start()

    @pl.when(c == 1)
    def _():
        o_copy(0, 0).start()

    @pl.when(c == 0)
    def _():
        orr[y] = os[0, 0]

    loads[4].wait()
    for b in range(1, NY):
        send(os.at[0, 0], orr.at[b], oss.at[0, 0], osr.at[b], other).wait_recv()

    @pl.when(c == 1)
    def _():
        send(os.at[0, 0], orr.at[0], oss.at[0, 0], osr.at[0], other).wait_recv()

    @pl.loop(0, S)
    def _(s):
        att = orr[:, s].reshape(D, B).T
        out_ref[s] = jnp.dot(att, wf[...], preferred_element_type=F32).astype(BF)

    for s in range(S):
        rows_over(s).wait_send()
        for d in range(1, NY):
            q_copy(s, d).wait_send()
    for half in range(2):
        for d in range(1, NY):
            for s in range(S):
                k_copy(half, s, d).wait_send()
                v_copy(half, s, d).wait_send()
        for rel in range(NY):
            k_forward(half, rel).wait_send()
            v_forward(half, rel).wait_send()
        for d in range(1, NX):
            x_copy(half, d).wait_send()
        for d in range(1, NZ):
            z_copy(half, d).wait_send()
    for d in range(1, NZ):
        pz_copy(d).wait_send()
    for d in range(1, NX):
        px_copy(d).wait_send()
    for slot, k in ((1, 0), (1, 1), (0, 1)):
        o_copy(slot, k).wait_send()

    @pl.when(c == 1)
    def _():
        o_copy(0, 0).wait_send()
        for s in range(S):
            q_copy(s, 0).wait_send()


def body(rows, gain, wq, wk, wv, wf):
    slab = (S, H, E, B)
    dma = pltpu.SemaphoreType.DMA
    scratch = [
        pltpu.VMEM((S, B, D), BF), pltpu.VMEM((S, B, D), BF), pltpu.VMEM((S, B, D), BF),
        pltpu.VMEM((D, D), BF), pltpu.VMEM((D, D), BF), pltpu.VMEM((D, D), BF), pltpu.VMEM((D, D), BF),
        pltpu.VMEM((NY,) + slab, BF), pltpu.VMEM((2, NY) + slab, BF), pltpu.VMEM((2, NY) + slab, BF),
        pltpu.VMEM((2, 2) + slab, BF), pltpu.VMEM((2, NY, 2) + slab, BF), pltpu.VMEM((2, NY, 2) + slab, BF),
        pltpu.VMEM((H, ROWS, 2 * S * E), BF),
        pltpu.VMEM((2, NX, H, ROWS // NX, HALF), BF), pltpu.VMEM((2, NX - 1, H, ROWS // NX, HALF), BF),
        pltpu.VMEM((2, NZ, H, ROWS // NX // NZ, HALF), BF), pltpu.VMEM((2, NZ - 1, H, ROWS // NX // NZ, HALF), BF),
        pltpu.VMEM((NX, NZ, H, ROWS // NX // NZ, 2 * HALF), BF),
        pltpu.VMEM((2, 2) + slab, BF), pltpu.VMEM((NY,) + slab, BF),
        dma((5,)), dma((S,)), dma((S,)),
        dma((NY, S)), dma((2, 2, S)),
        dma((2, NY - 1, S)), dma((2, NY - 1, S)), dma((2, NY - 1, S)), dma((2, NY - 1, S)),
        dma((2, NY)), dma((2, NY)), dma((2, NY)), dma((2, NY)),
        dma((2, NX - 1)), dma((2, NX - 1)), dma((2, NZ - 1)), dma((2, NZ - 1)),
        dma((NZ - 1,)), dma((NZ - 1,)), dma((NX - 1,)), dma((NX - 1,)),
        dma((2, 2)), dma((NY,)),
    ]
    anywhere = pl.BlockSpec(memory_space=pl.ANY)
    vmem = pl.BlockSpec(memory_space=pltpu.VMEM)
    return pl.pallas_call(
        kernel,
        out_shape=jax.ShapeDtypeStruct((S, B, D), BF),
        in_specs=[anywhere, vmem, anywhere, anywhere, anywhere, anywhere],
        out_specs=vmem,
        scratch_shapes=scratch,
        compiler_params=pltpu.CompilerParams(
            collective_id=0, has_side_effects=True, vmem_limit_bytes=56 * 1024 * 1024
        ),
        name="tied_row_attention",
    )(rows, gain.reshape(1, D), wq, wk, wv, wf)


def solution(mesh):
    placed = (P("seq", "res", None), P(), P(), P(), P(), P())
    return jax.shard_map(
        body, mesh=mesh, in_specs=placed, out_specs=P("seq", "res", None), check_vma=False
    )
```

time: 391 us -> 106 us (0.27)
  waiting for transfers between devices: 256 us -> 0 us
  Pallas kernels: 0 us -> 103 us
  blocking collectives: 79.5 us -> 0 us
  local copies, waits for them, and re-layouts: 21.8 us -> 3.18 us
  between operations: 13.5 us -> 0.01 us
  matrix products: 12.4 us -> 0 us
  other arithmetic: 5.83 us -> 0 us
    all_gather x2 -> x0, waiting for transfers between devices: 256 us -> none  [the longest x1 197 us: side_by_side(): out = lax.all_gather(both, axis, axis=dim, tiled=True)]
    pallas_call x0 -> x1, Pallas kernels: none -> 103 us  [body(): pl.pallas_call(kernel, out_shape=jax.ShapeDtypeStruct((S, B, D), BF), in_...]
    all_to_all x1 -> x0, blocking collectives: 79.5 us -> none  [sent_and_summed(): lax.all_to_all(parts, axis, split_axis=0, concat_axis=0, tiled=True)]
    dot_general x6 -> x0, matrix products: 12.4 us -> none  [the longest x1 6.22 us: body(): jnp.einsum('hij,sjhe->sihe', probs, content_array, preferred_element_type...]
    reshape x5 -> x1, local copies, waits for them, and re-layouts: 10.9 us -> 1.27 us  [body(): gain.reshape(1, D)]
    split x1 -> x0, local copies, waits for them, and re-layouts: 7.17 us -> none  [side_by_side(): jnp.split(out, [sum(widths[:k]) for k in range(1, len(widths))], axis=along)]
    reduce_sum x3 -> x0, other arithmetic: 4.11 us -> none  [the longest x1 1.39 us: sent_and_summed(): return arrived.astype(jnp.float32).sum(axis=0)]
  transfers between devices with their start and end apart: 2 -> 0, of which waited for: 2 -> 0; matrix products, arithmetic and copies ran while one was open for 0% -> 0% of each run, Pallas kernels for 0% -> 0%
where the time goes in v1:
time: 106 us
  Pallas kernels  103 us (97%)
  local copies, waits for them, and re-layouts  3.18 us (3%)
    pallas_call x1, Pallas kernels, body(): pl.pallas_call(kernel, out_shape=jax.ShapeDtypeStruct((S, B, D), BF), in_...  103 us

profile of v1, /device:TPU:33, one launch (start us, length us, event | category | flops | bytes accessed | tf_op | source)
XLA Modules:
  0.0 105.8 jit_solution(13136803412095648074)
XLA Ops:
  0.0 1.3 %reshape.3.gain_ref = f32[1,768]{1,0:T(1,128)} reshape(f32[768]{0:T(1024)} %param.7) | data formatting | bytes 6144 | tf_op jit(solution)/shard_map/reshape | solution.py:367
  1.3 102.6 %tied_row_attention.1 = bf16[3,128,768]{2,1,0:T(8,128)(2,1)} custom-call(bf16[3,128,768]{2,1,0:T(8,128)(2,1)} %x_hbm.1, f32[1,768]{1,0:T(1,128)} %reshape.3.gain_ref, bf16[768,768]{1,0:T(8,128)(2,1)} %wq_hbm.1, bf16[768,768]{1,0:T(8,128)(2,1)} %wk_hbm.1, bf16[768,768]{1,0:T(8,128)(2,1)} %wv_hbm.1, bf16[768,768]{1,0:T(8,128)(2,1)} %wf_hbm.1), custom_call_target="tpu_custom_call" | custom-call | tf_op jit(solution)/shard_map/tied_row_attention/pallas_call | solution.py:357
  103.9 1.9 %copy.8 = bf16[3,128,768]{2,1,0:T(8,128)(2,1)} copy(bf16[3,128,768]{2,1,0:T(8,128)(2,1)} %tied_row_attention.1) | data formatting | bytes 1179648

commit v2 on v1

v2 whole, which is shorter than its diff:
```python
import functools

import jax
import jax.numpy as jnp
from jax import lax
from jax.experimental import pallas as pl
from jax.experimental.pallas import tpu as pltpu
from jax.sharding import PartitionSpec as P

MESH = pl.DeviceIdType.MESH
BF = jnp.bfloat16
F32 = jnp.float32
NX, NY, NZ = 4, 4, 4
S, B, D = 3, 128, 768
H, E = 3, 64
ROWS = 256
HALF = NY * B
SHARE = ROWS // NX // NZ


def kernel(
    x_hbm, gain_ref, wq_hbm, wk_hbm, wv_hbm, out_ref,
    xo, xp, xn, wq, wk, wv, qt, kt, vt, qr, kr, vr, qn, xs, xr, zs, zr, pf, ff, os, orr,
    lsem, zss, zrs, qss, qrs, kss, krs, vss, vrs, kfs, kfr, vfs, vfr,
    xss, xrs, lss, lrs, pzs, pzr, pxs, pxr, fzs, fzr, fxs, fxr, oss, osr,
):
    seq, res = lax.axis_index("seq"), lax.axis_index("res")
    c, x, zl = lax.rem(seq, 2), lax.rem(seq // 2, NX), seq // (2 * NX)
    y, zh = lax.rem(res, NY), res // NY

    def dev(x=x, zl=zl, c=c, y=y, zh=zh):
        return ((zl * NX + x) * 2 + c, zh * NY + y)

    def up(i, d, n):
        return lax.rem(i + d, n)

    other = dev(c=1 - c)

    def send(src, dst, ss, rs, to):
        return pltpu.make_async_remote_copy(
            src_ref=src, dst_ref=dst, send_sem=ss, recv_sem=rs, device_id=to, device_id_type=MESH
        )

    loads = [
        pltpu.make_async_copy(a, b, lsem.at[i])
        for i, (a, b) in enumerate(((x_hbm, xo), (wq_hbm, wq), (wk_hbm, wk), (wv_hbm, wv)))
    ]
    for copy in loads:
        copy.start()

    barrier = pltpu.get_barrier_semaphore()
    peers = [other, dev(zh=1 - zh)]
    peers += [dev(x=up(x, d, NX)) for d in range(1, NX)]
    peers += [dev(zl=up(zl, d, NZ)) for d in range(1, NZ)]
    peers += [dev(y=up(y, d, NY), c=k) for d in range(1, NY) for k in range(2)]
    for peer in peers:
        pl.semaphore_signal(barrier, inc=1, device_id=peer, device_id_type=MESH)
    pl.semaphore_wait(barrier, len(peers))

    loads[0].wait()

    def rows_over(s):
        return send(xo.at[s], xp.at[s], zss.at[s], zrs.at[s], dev(zh=1 - zh))

    for s in range(S):
        rows_over(s).start()

    def norm(rows):
        rows = rows.astype(F32)
        center = rows - jnp.mean(rows, axis=-1, keepdims=True)
        spread = jnp.mean(center * center, axis=-1, keepdims=True)
        return (center * lax.rsqrt(spread + 1e-05) * gain_ref[...].reshape(1, D)).astype(BF)

    def project(normed, w):
        out = jnp.dot(normed, w[...], preferred_element_type=F32).astype(BF)
        return out.T.reshape(NY, H, E, B)

    def q_copy(s, d):
        b = (-d) % NY
        to = dev(y=up(y, d, NY), c=b // 2)
        return send(qt.at[up(y, d, NY), s], qr.at[b % 2, c, s], qss.at[d, s], qrs.at[b % 2, c, s], to)

    def kv_copy(t, r, ss, rs, half, s, d):
        g = up(y, d, NY)
        return send(
            t.at[half, g, s], r.at[half, (-d) % NY, c, s], ss.at[half, d - 1, s], rs.at[half, d - 1, s], dev(y=g)
        )

    def forward(r, ss, rs, half, rel):
        part = r.at[half, rel, c]
        return send(part, part, ss.at[half, rel], rs.at[half, rel], other)

    k_copy = functools.partial(kv_copy, kt, kr, kss, krs)
    v_copy = functools.partial(kv_copy, vt, vr, vss, vrs)
    k_forward = functools.partial(forward, kr, kfs, kfr)
    v_forward = functools.partial(forward, vr, vfs, vfr)

    for copy in loads[1:3]:
        copy.wait()

    @pl.loop(0, S)
    def _(s):
        normed = norm(xo[s])
        xn[s] = normed
        qt[:, s] = project(normed, wq)
        kt[0, :, s] = project(normed, wk)
        for d in range(1, NY):
            q_copy(s, d).start()

        @pl.when(c == 1)
        def _():
            q_copy(s, 0).start()

        @pl.when(c == 0)
        def _():
            qr[0, 0, s] = qt[y, s]

        for d in range(1, NY):
            k_copy(0, s, d).start()
        kr[0, 0, c, s] = kt[0, y, s]

    k_forward(0, 0).start()
    loads[3].wait()

    @pl.loop(0, S)
    def _(s):
        v = project(xn[s], wv)
        vt[0, :, s] = v
        vr[0, 0, c, s] = vt[0, y, s]

    v_forward(0, 0).start()

    def partner(s):
        rows_over(s).wait_recv()
        normed = norm(xp[s])
        kt[1, :, s] = project(normed, wk)
        for d in range(1, NY):
            k_copy(1, s, d).start()
        kr[1, 0, c, s] = kt[1, y, s]
        vt[1, :, s] = project(normed, wv)
        vr[1, 0, c, s] = vt[1, y, s]

    def forward_all(copy, fwd, half):
        for d in range(1, NY):
            for s in range(S):
                copy(half, s, d).wait_recv()
            fwd(half, (-d) % NY).start()

    def columns(r, half, h):
        return jnp.concatenate(
            [r[half, rel, :, :, h].reshape(2 * S * E, B) for rel in range(NY)], axis=1
        )

    def x_copy(half, h, d):
        g = up(x, d, NX)
        at = (half, h, d - 1)
        return send(xs.at[half, h, g], xr.at[at], xss.at[at], xrs.at[at], dev(x=g))

    def z_copy(half, h, d):
        g = up(zl, d, NZ)
        at = (half, h, d - 1)
        return send(zs.at[half, h, g], zr.at[at], lss.at[at], lrs.at[at], dev(zl=g))

    def pz_copy(half, h, d):
        part, at = pf.at[half, h, x, zl], (half, h, d - 1)
        return send(part, part, pzs.at[at], pzr.at[at], dev(zl=up(zl, d, NZ)))

    def px_copy(half, h, d):
        part, at = pf.at[half, h, x], (half, h, d - 1)
        return send(part, part, pxs.at[at], pxr.at[at], dev(x=up(x, d, NX)))

    def fz_copy(d):
        part = ff.at[x, zl]
        return send(part, part, fzs.at[d - 1], fzr.at[d - 1], dev(zl=up(zl, d, NZ)))

    def fx_copy(d):
        part = ff.at[x]
        return send(part, part, fxs.at[d - 1], fxr.at[d - 1], dev(x=up(x, d, NX)))

    def logits(half):
        for rel in range(NY):
            k_forward(half, rel).wait_recv()

        @pl.loop(0, H)
        def _(h):
            part = jnp.dot(qn[h], columns(kr, half, h), preferred_element_type=F32).astype(BF)
            xs[half, h] = part.reshape(NX, ROWS // NX, HALF)
            for d in range(1, NX):
                x_copy(half, h, d).start()

    def over_x(half, h):
        for d in range(1, NX):
            x_copy(half, h, d).wait_recv()
        total = xs[half, h, x].astype(F32)
        for d in range(1, NX):
            total += xr[half, h, d - 1].astype(F32)
        zs[half, h] = total.astype(BF).reshape(NZ, SHARE, HALF)
        for d in range(1, NZ):
            z_copy(half, h, d).start()

    def over_z(half, h):
        for d in range(1, NZ):
            z_copy(half, h, d).wait_recv()
        total = zs[half, h, zl].astype(F32)
        for d in range(1, NZ):
            total += zr[half, h, d - 1].astype(F32)
        return total

    scale = 1.0 / (8.0 * (96.0**0.5))
    tops, sums, factors = [], [], []

    def near(h):
        total = over_z(0, h)
        top = jnp.max(total, axis=-1, keepdims=True)
        weights = jnp.exp((total - top) * scale)
        tops.append(top)
        sums.append(jnp.sum(weights, axis=-1, keepdims=True))
        pf[0, h, x, zl] = weights.astype(BF)
        for d in range(1, NZ):
            pz_copy(0, h, d).start()

    def far(h):
        total = over_z(1, h)
        top = jnp.maximum(tops[h], jnp.max(total, axis=-1, keepdims=True))
        weights = jnp.exp((total - top) * scale)
        old = jnp.exp((tops[h] - top) * scale)
        inverse = 1.0 / (old * sums[h] + jnp.sum(weights, axis=-1, keepdims=True))
        factors.append(old * inverse)
        pf[1, h, x, zl] = (weights * inverse).astype(BF)
        for d in range(1, NZ):
            pz_copy(1, h, d).start()

    def pass_on(half, h):
        for d in range(1, NZ):
            pz_copy(half, h, d).wait_recv()
        for d in range(1, NX):
            px_copy(half, h, d).start()

    partner(0)
    forward_all(k_copy, k_forward, 0)
    for b, k in ((0, 1), (1, 0), (1, 1)):
        for s in range(S):
            send(qt.at[0, s], qr.at[b, k, s], qss.at[0, s], qrs.at[b, k, s], other).wait_recv()

    @pl.when(c == 1)
    def _():
        for s in range(S):
            send(qt.at[0, s], qr.at[0, 0, s], qss.at[0, s], qrs.at[0, 0, s], other).wait_recv()

    @pl.loop(0, H)
    def _(h):
        cols = [qr[b, :, :, h].reshape(2 * S * E, B).T for b in range(2)]
        qn[h] = jnp.concatenate(cols, axis=0)

    logits(0)
    partner(1)
    over_x(0, 0)
    partner(2)
    k_forward(1, 0).start()
    v_forward(1, 0).start()

    @pl.loop(0, 2)
    def _(half):
        @pl.loop(0, S)
        def _(s):
            for d in range(1, NY):
                v_copy(half, s, d).start()

    over_x(0, 1)
    over_x(0, 2)
    forward_all(k_copy, k_forward, 1)
    logits(1)
    for h in range(H):
        near(h)
    for h in range(H):
        pass_on(0, h)
    over_x(1, 0)
    over_x(1, 1)
    far(0)
    over_x(1, 2)
    far(1)
    forward_all(v_copy, v_forward, 0)
    pass_on(1, 0)
    far(2)
    lane = lax.broadcasted_iota(jnp.int32, (SHARE, B), 1)
    ff[x, zl] = jnp.where(lane == 0, factors[0], jnp.where(lane == 1, factors[1], factors[2]))
    for d in range(1, NZ):
        fz_copy(d).start()
    pass_on(1, 1)
    forward_all(v_copy, v_forward, 1)
    pass_on(1, 2)
    for d in range(1, NZ):
        fz_copy(d).wait_recv()
    for d in range(1, NX):
        fx_copy(d).start()
    for half in range(2):
        for rel in range(NY):
            v_forward(half, rel).wait_recv()

    def o_copy(slot, k, h):
        b = 2 * c + slot
        return send(
            os.at[slot, k, h], orr.at[y, h], oss.at[slot, k, h], osr.at[b, h], dev(y=up(y, b, NY), c=k)
        )

    for d in range(1, NX):
        fx_copy(d).wait_recv()

    @pl.loop(0, H)
    def _(h):
        for half in range(2):
            for d in range(1, NX):
                px_copy(half, h, d).wait_recv()
        factor = jnp.sum(
            jnp.where(lax.broadcasted_iota(jnp.int32, (ROWS, B), 1) == h, ff[...].reshape(ROWS, B), 0.0),
            axis=-1,
            keepdims=True,
        )
        weights = [
            (pf[0, h].reshape(ROWS, HALF).astype(F32) * factor).astype(BF),
            pf[1, h].reshape(ROWS, HALF),
        ]
        total = jnp.zeros((2 * S * E, ROWS), F32)
        for half in range(2):
            total += lax.dot_general(
                columns(vr, half, h),
                weights[half],
                (((1,), (1,)), ((), ())),
                preferred_element_type=F32,
            )
        total = total.astype(BF)
        for b in range(2):
            os[b, :, h] = total[:, b * B : (b + 1) * B].reshape(2, S, E, B)
        for slot, k in ((1, 0), (1, 1), (0, 1)):
            o_copy(slot, k, h).start()

        @pl.when(c == 1)
        def _():
            o_copy(0, 0, h).start()

        @pl.when(c == 0)
        def _():
            orr[y, h] = os[0, 0, h]

    for h in range(H):
        for b in range(1, NY):
            send(os.at[0, 0, h], orr.at[b, h], oss.at[0, 0, h], osr.at[b, h], other).wait_recv()

    @pl.when(c == 1)
    def _():
        for h in range(H):
            send(os.at[0, 0, h], orr.at[0, h], oss.at[0, 0, h], osr.at[0, h], other).wait_recv()

    @pl.loop(0, S)
    def _(s):
        out_ref[s] = orr[:, :, s].reshape(D, B).T

    for s in range(S):
        rows_over(s).wait_send()
        for d in range(1, NY):
            q_copy(s, d).wait_send()
    for half in range(2):
        for d in range(1, NY):
            for s in range(S):
                k_copy(half, s, d).wait_send()
                v_copy(half, s, d).wait_send()
        for rel in range(NY):
            k_forward(half, rel).wait_send()
            v_forward(half, rel).wait_send()
        for h in range(H):
            for d in range(1, NX):
                x_copy(half, h, d).wait_send()
                px_copy(half, h, d).wait_send()
            for d in range(1, NZ):
                z_copy(half, h, d).wait_send()
                pz_copy(half, h, d).wait_send()
    for d in range(1, NZ):
        fz_copy(d).wait_send()
    for d in range(1, NX):
        fx_copy(d).wait_send()
    for h in range(H):
        for slot, k in ((1, 0), (1, 1), (0, 1)):
            o_copy(slot, k, h).wait_send()

    @pl.when(c == 1)
    def _():
        for h in range(H):
            o_copy(0, 0, h).wait_send()
        for s in range(S):
            q_copy(s, 0).wait_send()


def body(rows, gain, wq, wk, wv, wf):
    slab = (S, H, E, B)
    dma = pltpu.SemaphoreType.DMA
    scratch = [
        pltpu.VMEM((S, B, D), BF), pltpu.VMEM((S, B, D), BF), pltpu.VMEM((S, B, D), BF),
        pltpu.VMEM((D, D), BF), pltpu.VMEM((D, D), BF), pltpu.VMEM((D, D), BF),
        pltpu.VMEM((NY,) + slab, BF), pltpu.VMEM((2, NY) + slab, BF), pltpu.VMEM((2, NY) + slab, BF),
        pltpu.VMEM((2, 2) + slab, BF), pltpu.VMEM((2, NY, 2) + slab, BF), pltpu.VMEM((2, NY, 2) + slab, BF),
        pltpu.VMEM((H, ROWS, 2 * S * E), BF),
        pltpu.VMEM((2, H, NX, ROWS // NX, HALF), BF), pltpu.VMEM((2, H, NX - 1, ROWS // NX, HALF), BF),
        pltpu.VMEM((2, H, NZ, SHARE, HALF), BF), pltpu.VMEM((2, H, NZ - 1, SHARE, HALF), BF),
        pltpu.VMEM((2, H, NX, NZ, SHARE, HALF), BF), pltpu.VMEM((NX, NZ, SHARE, B), F32),
        pltpu.VMEM((2, 2, H, S, E, B), BF), pltpu.VMEM((NY, H, S, E, B), BF),
        dma((4,)), dma((S,)), dma((S,)),
        dma((NY, S)), dma((2, 2, S)),
        dma((2, NY - 1, S)), dma((2, NY - 1, S)), dma((2, NY - 1, S)), dma((2, NY - 1, S)),
        dma((2, NY)), dma((2, NY)), dma((2, NY)), dma((2, NY)),
        dma((2, H, NX - 1)), dma((2, H, NX - 1)), dma((2, H, NZ - 1)), dma((2, H, NZ - 1)),
        dma((2, H, NZ - 1)), dma((2, H, NZ - 1)), dma((2, H, NX - 1)), dma((2, H, NX - 1)),
        dma((NZ - 1,)), dma((NZ - 1,)), dma((NX - 1,)), dma((NX - 1,)),
        dma((2, 2, H)), dma((NY, H)),
    ]
    anywhere = pl.BlockSpec(memory_space=pl.ANY)
    vmem = pl.BlockSpec(memory_space=pltpu.VMEM)
    attended = pl.pallas_call(
        kernel,
        out_shape=jax.ShapeDtypeStruct((S, B, D), BF),
        in_specs=[anywhere, vmem, anywhere, anywhere, anywhere],
        out_specs=vmem,
        scratch_shapes=scratch,
        compiler_params=pltpu.CompilerParams(
            collective_id=0, has_side_effects=True, vmem_limit_bytes=56 * 1024 * 1024
        ),
        name="tied_row_attention",
    )(rows, gain, wq, wk, wv)
    mixed = jnp.dot(attended.reshape(S * B, D), wf, preferred_element_type=F32).astype(BF)
    return mixed.reshape(S, B, D)


def solution(mesh):
    placed = (P("seq", "res", None), P(), P(), P(), P(), P())
    return jax.shard_map(
        body, mesh=mesh, in_specs=placed, out_specs=P("seq", "res", None), check_vma=False
    )
```

time: 106 us -> 90.8 us (0.86)
  Pallas kernels: 103 us -> 88.1 us
  local copies, waits for them, and re-layouts: 3.18 us -> 0.01 us
  matrix products: 0 us -> 2.51 us
    pallas_call x1, Pallas kernels: 103 us -> 88.1 us  [body(): pl.pallas_call(kernel, out_shape=jax.ShapeDtypeStruct((S, B, D), BF), in_...]
    dot_general x0 -> x1, matrix products: none -> 2.51 us  [body(): jnp.dot(attended.reshape(S * B, D), wf, preferred_element_type=F32)]
    unnamed x1 -> x2, local copies, waits for them, and re-layouts: 1.92 us -> 0.01 us
    reshape x1 -> x0, local copies, waits for them, and re-layouts: 1.27 us -> none  [body(): gain.reshape(1, D)]
where the time goes in v2:
time: 90.8 us; the launch traced here: 90.6 us
  Pallas kernels  88.1 us (97%)
  matrix products  2.51 us (3%)
    pallas_call x1, Pallas kernels, body(): pl.pallas_call(kernel, out_shape=jax.ShapeDtypeStruct((S, B, D), BF), in_...  88.1 us
    dot_general x1, matrix products, body(): jnp.dot(attended.reshape(S * B, D), wf, preferred_element_type=F32)  2.51 us

profile of v2, /device:TPU:33, one launch (start us, length us, event | category | flops | bytes accessed | tf_op | source)
XLA Modules:
  0.0 90.6 jit_solution(3328535428821878430)
XLA Ops:
  0.0 0.0 copy-start
  0.0 88.1 %tied_row_attention.1 = bf16[3,128,768]{2,1,0:T(8,128)(2,1)} custom-call(bf16[3,128,768]{2,1,0:T(8,128)(2,1)} %x_hbm.1, f32[768]{0:T(1024)} %gain_ref.1, bf16[768,768]{1,0:T(8,128)(2,1)} %wq_hbm.1, bf16[768,768]{1,0:T(8,128)(2,1)} %wk_hbm.1, bf16[768,768]{1,0:T(8,128)(2,1)} %wv_hbm.1), custom_call_target="tpu_custom_call" | custom-call | tf_op jit(solution)/shard_map/tied_row_attention/pallas_call | solution.py:417
  88.1 0.0 copy-done
  88.1 2.5 %convolution_convert_fusion = bf16[384,768]{1,0:T(8,128)(2,1)} fusion(bf16[384,768]{1,0:T(8,128)(2,1)} %bitcast.4, bf16[768,768]{1,0:T(8,128)(2,1)S(1)} %copy-done), kind=kOutput, calls=%fused_computation | convolution fusion | flops 453279744 | bytes 2359296 | tf_op jit(solution)/shard_map/dot_general | solution.py:428
Async XLA Ops:
  0.0 88.1 %copy-start = (bf16[768,768]{1,0:T(8,128)(2,1)S(1)}, bf16[768,768]{1,0:T(8,128)(2,1)}, u32[]{:S(2)}) copy-start(bf16[768,768]{1,0:T(8,128)(2,1)} %param.11) | copy-start | bytes 3538948

commit v3 on v2

v3 whole, which is shorter than its diff:
```python
import functools

import jax
import jax.numpy as jnp
from jax import lax
from jax.experimental import pallas as pl
from jax.experimental.pallas import tpu as pltpu
from jax.sharding import PartitionSpec as P

MESH = pl.DeviceIdType.MESH
BF = jnp.bfloat16
F32 = jnp.float32
NX, NY, NZ = 4, 4, 4
S, B, D = 3, 128, 768
H, E = 3, 64
ROWS = 256
HALF = NY * B
SHARE = ROWS // NX // NZ


def kernel(
    x_hbm, gain_ref, wq_hbm, wk_hbm, wv_hbm, out_ref,
    xo, xp, xn, wq, wk, wv, qt, kt, vt, qr, kr, vr, qn, xs, xr, zs, zr, pf, fz, ff, os, orr,
    lsem, zss, zrs, qss, qrs, kss, krs, vss, vrs, kfs, kfr, vfs, vfr,
    xss, xrs, lss, lrs, pzs, pzr, pxs, pxr, fzs, fzr, fxs, fxr, oss, osr,
):
    seq, res = lax.axis_index("seq"), lax.axis_index("res")
    c, x, zl = lax.rem(seq, 2), lax.rem(seq // 2, NX), seq // (2 * NX)
    y, zh = lax.rem(res, NY), res // NY

    def dev(x=x, zl=zl, c=c, y=y, zh=zh):
        return ((zl * NX + x) * 2 + c, zh * NY + y)

    def up(i, d, n):
        return lax.rem(i + d, n)

    other = dev(c=1 - c)

    def send(src, dst, ss, rs, to):
        return pltpu.make_async_remote_copy(
            src_ref=src, dst_ref=dst, send_sem=ss, recv_sem=rs, device_id=to, device_id_type=MESH
        )

    loads = [
        pltpu.make_async_copy(a, b, lsem.at[i])
        for i, (a, b) in enumerate(((x_hbm, xo), (wq_hbm, wq), (wk_hbm, wk), (wv_hbm, wv)))
    ]
    for copy in loads:
        copy.start()

    barrier = pltpu.get_barrier_semaphore()
    peers = [other, dev(zh=1 - zh)]
    peers += [dev(x=up(x, d, NX)) for d in range(1, NX)]
    peers += [dev(zl=up(zl, d, NZ)) for d in range(1, NZ)]
    peers += [dev(y=up(y, d, NY), c=k) for d in range(1, NY) for k in range(2)]
    for peer in peers:
        pl.semaphore_signal(barrier, inc=1, device_id=peer, device_id_type=MESH)
    pl.semaphore_wait(barrier, len(peers))

    loads[0].wait()

    def landed(ref, rs):
        send(ref, ref, rs, rs, other).wait_recv()

    def left(ref, ss):
        send(ref, ref, ss, ss, other).wait_send()

    def rows_over(s):
        return send(xo.at[s], xp.at[s], zss, zrs.at[s], dev(zh=1 - zh))

    for s in range(S):
        rows_over(s).start()

    def norm(rows):
        rows = rows.astype(F32)
        center = rows - jnp.mean(rows, axis=-1, keepdims=True)
        spread = jnp.mean(center * center, axis=-1, keepdims=True)
        return (center * lax.rsqrt(spread + 1e-05) * gain_ref[...].reshape(1, D)).astype(BF)

    def project(normed, w):
        out = jnp.dot(normed, w[...], preferred_element_type=F32).astype(BF)
        return out.T.reshape(NY, H, E, B)

    def q_copy(s, d):
        b = (-d) % NY
        to = dev(y=up(y, d, NY), c=b // 2)
        return send(qt.at[up(y, d, NY), s], qr.at[b % 2 * 2 + c, s], qss, qrs, to)

    def kv_copy(t, r, ss, rs, half, s, d):
        g = up(y, d, NY)
        return send(t.at[half, g, s], r.at[half, (-d) % NY, c, s], ss, rs.at[half, d - 1], dev(y=g))

    def forward(r, ss, rs, half, rel):
        part = r.at[half, rel, c]
        return send(part, part, ss, rs.at[half], other)

    k_copy = functools.partial(kv_copy, kt, kr, kss, krs)
    v_copy = functools.partial(kv_copy, vt, vr, vss, vrs)
    k_forward = functools.partial(forward, kr, kfs, kfr)
    v_forward = functools.partial(forward, vr, vfs, vfr)

    for copy in loads[1:3]:
        copy.wait()

    @pl.loop(0, S)
    def _(s):
        normed = norm(xo[s])
        xn[s] = normed
        qt[:, s] = project(normed, wq)
        kt[0, :, s] = project(normed, wk)
        for d in range(1, NY):
            q_copy(s, d).start()

        @pl.when(c == 1)
        def _():
            q_copy(s, 0).start()

        @pl.when(c == 0)
        def _():
            qr[0, s] = qt[y, s]

        for d in range(1, NY):
            k_copy(0, s, d).start()
        kr[0, 0, c, s] = kt[0, y, s]

    k_forward(0, 0).start()
    loads[3].wait()

    @pl.loop(0, S)
    def _(s):
        v = project(xn[s], wv)
        vt[0, :, s] = v
        vr[0, 0, c, s] = vt[0, y, s]

    v_forward(0, 0).start()

    def partner(s):
        rows_over(s).wait_recv()
        normed = norm(xp[s])
        kt[1, :, s] = project(normed, wk)
        for d in range(1, NY):
            k_copy(1, s, d).start()
        kr[1, 0, c, s] = kt[1, y, s]
        vt[1, :, s] = project(normed, wv)
        vr[1, 0, c, s] = vt[1, y, s]

    def forward_all(r, rs, fwd, half):
        for d in range(1, NY):
            landed(r.at[half, (-d) % NY, c], rs.at[half, d - 1])
            fwd(half, (-d) % NY).start()

    def columns(r, half, h):
        return jnp.concatenate(
            [r[half, rel, :, :, h].reshape(2 * S * E, B) for rel in range(NY)], axis=1
        )

    def x_copy(half, h, d):
        g = up(x, d, NX)
        return send(xs.at[half, h, g], xr.at[half, h, d - 1], xss, xrs.at[half, h], dev(x=g))

    def z_copy(half, h, d):
        g = up(zl, d, NZ)
        return send(zs.at[half, h, g], zr.at[half, h, d - 1], lss, lrs.at[half, h], dev(zl=g))

    def pz_copy(half, h, d):
        part = pf.at[half, h, x, zl]
        return send(part, part, pzs, pzr.at[half, h], dev(zl=up(zl, d, NZ)))

    def px_copy(half, h, d):
        part = pf.at[half, h, x]
        return send(part, part, pxs, pxr.at[h], dev(x=up(x, d, NX)))

    def fz_copy(h, d):
        part = fz.at[h, zl]
        return send(part, part, fzs, fzr.at[h], dev(zl=up(zl, d, NZ)))

    def fx_copy(h, d):
        part = ff.at[h, x]
        return send(part, part, fxs, fxr.at[h], dev(x=up(x, d, NX)))

    def logits(half):
        landed(kr.at[half, :, c], kfr.at[half])

        @pl.loop(0, H)
        def _(h):
            part = jnp.dot(qn[h], columns(kr, half, h), preferred_element_type=F32).astype(BF)
            xs[half, h] = part.reshape(NX, ROWS // NX, HALF)
            for d in range(1, NX):
                x_copy(half, h, d).start()

    def over_x(half, h):
        landed(xr.at[half, h], xrs.at[half, h])
        total = xs[half, h, x].astype(F32)
        for d in range(1, NX):
            total += xr[half, h, d - 1].astype(F32)
        zs[half, h] = total.astype(BF).reshape(NZ, SHARE, HALF)
        for d in range(1, NZ):
            z_copy(half, h, d).start()

    def over_z(half, h):
        landed(zr.at[half, h], lrs.at[half, h])
        total = zs[half, h, zl].astype(F32)
        for d in range(1, NZ):
            total += zr[half, h, d - 1].astype(F32)
        return total

    scale = 1.0 / (8.0 * (96.0**0.5))
    tops, sums = [], []
    lane = lax.broadcasted_iota(jnp.int32, (SHARE, B), 1)

    def near(h):
        total = over_z(0, h)
        top = jnp.max(total, axis=-1, keepdims=True)
        weights = jnp.exp((total - top) * scale)
        tops.append(top)
        sums.append(jnp.sum(weights, axis=-1, keepdims=True))
        pf[0, h, x, zl] = weights.astype(BF)
        for d in range(1, NZ):
            pz_copy(0, h, d).start()

    def far(h):
        total = over_z(1, h)
        top = jnp.maximum(tops[h], jnp.max(total, axis=-1, keepdims=True))
        weights = jnp.exp((total - top) * scale)
        old = jnp.exp((tops[h] - top) * scale)
        inverse = 1.0 / (old * sums[h] + jnp.sum(weights, axis=-1, keepdims=True))
        fz[h, zl] = jnp.broadcast_to(old * inverse, (SHARE, B))
        pf[1, h, x, zl] = (weights * inverse).astype(BF)
        for d in range(1, NZ):
            fz_copy(h, d).start()
            pz_copy(1, h, d).start()

    def pass_on(half, h):
        if half:
            landed(fz.at[h, pl.ds(0, NZ - 1)], fzr.at[h])
            packed = fz[h, 0]
            for k in range(1, NZ):
                packed = jnp.where(lane == k, fz[h, k], packed)
            ff[h, x] = packed
            for d in range(1, NX):
                fx_copy(h, d).start()
        landed(pf.at[half, h, x, pl.ds(0, NZ - 1)], pzr.at[half, h])
        for d in range(1, NX):
            px_copy(half, h, d).start()

    partner(0)
    forward_all(kr, krs, k_forward, 0)
    @pl.when(c == 0)
    def _():
        landed(qr.at[pl.ds(1, 3)], qrs)

    @pl.when(c == 1)
    def _():
        landed(qr, qrs)

    @pl.loop(0, H)
    def _(h):
        cols = [qr[2 * b : 2 * b + 2, :, h].reshape(2 * S * E, B).T for b in range(2)]
        qn[h] = jnp.concatenate(cols, axis=0)

    logits(0)
    partner(1)
    over_x(0, 0)
    partner(2)
    k_forward(1, 0).start()
    v_forward(1, 0).start()

    @pl.loop(0, 2)
    def _(half):
        @pl.loop(0, S)
        def _(s):
            for d in range(1, NY):
                v_copy(half, s, d).start()

    over_x(0, 1)
    over_x(0, 2)
    forward_all(kr, krs, k_forward, 1)
    logits(1)
    for h in range(H):
        near(h)
    over_x(1, 0)
    for h in range(H):
        pass_on(0, h)
    over_x(1, 1)
    far(0)
    over_x(1, 2)
    far(1)
    forward_all(vr, vrs, v_forward, 0)
    pass_on(1, 0)
    far(2)
    pass_on(1, 1)
    forward_all(vr, vrs, v_forward, 1)
    pass_on(1, 2)
    for half in range(2):
        landed(vr.at[half, :, c], vfr.at[half])

    def o_copy(slot, k, h):
        b = 2 * c + slot
        return send(os.at[slot, k, h], orr.at[y, h], oss, osr, dev(y=up(y, b, NY), c=k))

    @pl.loop(0, H)
    def _(h):
        landed(ff.at[h, pl.ds(0, NX - 1)], fxr.at[h])
        landed(pf.at[:, h, pl.ds(0, NX - 1)], pxr.at[h])
        factor = jnp.concatenate([ff[h, i, :, k : k + 1] for i in range(NX) for k in range(NZ)], axis=0)
        weights = [
            (pf[0, h].reshape(ROWS, HALF).astype(F32) * factor).astype(BF),
            pf[1, h].reshape(ROWS, HALF),
        ]
        total = jnp.zeros((2 * S * E, ROWS), F32)
        for half in range(2):
            total += lax.dot_general(
                columns(vr, half, h),
                weights[half],
                (((1,), (1,)), ((), ())),
                preferred_element_type=F32,
            )
        total = total.astype(BF)
        for b in range(2):
            os[b, :, h] = total[:, b * B : (b + 1) * B].reshape(2, S, E, B)
        for slot, k in ((1, 0), (1, 1), (0, 1)):
            o_copy(slot, k, h).start()

        @pl.when(c == 1)
        def _():
            o_copy(0, 0, h).start()

        @pl.when(c == 0)
        def _():
            orr[y, h] = os[0, 0, h]

    @pl.when(c == 0)
    def _():
        landed(orr.at[pl.ds(1, 3)], osr)

    @pl.when(c == 1)
    def _():
        landed(orr, osr)

    @pl.loop(0, S)
    def _(s):
        out_ref[s] = orr[:, :, s].reshape(D, B).T

    left(xo, zss)
    left(kt.at[:, pl.ds(1, NY - 1)], kss)
    left(vt.at[:, pl.ds(1, NY - 1)], vss)
    left(kr.at[:, :, c], kfs)
    left(vr.at[:, :, c], vfs)
    left(xs.at[:, :, pl.ds(1, NX - 1)], xss)
    left(zs.at[:, :, pl.ds(1, NZ - 1)], lss)
    left(pf.at[:, :, 0, pl.ds(1, NZ - 1)], pzs)
    left(pf.at[:, :, pl.ds(1, NX - 1)], pxs)
    left(fz.at[:, pl.ds(1, NZ - 1)], fzs)
    left(ff.at[:, pl.ds(1, NX - 1)], fxs)

    @pl.when(c == 0)
    def _():
        left(qt.at[pl.ds(1, 3)], qss)
        left(orr.at[pl.ds(1, 3)], oss)

    @pl.when(c == 1)
    def _():
        left(qt, qss)
        left(orr, oss)


def body(rows, gain, wq, wk, wv, wf):
    slab = (S, H, E, B)
    dma = pltpu.SemaphoreType.DMA
    scratch = [
        pltpu.VMEM((S, B, D), BF), pltpu.VMEM((S, B, D), BF), pltpu.VMEM((S, B, D), BF),
        pltpu.VMEM((D, D), BF), pltpu.VMEM((D, D), BF), pltpu.VMEM((D, D), BF),
        pltpu.VMEM((NY,) + slab, BF), pltpu.VMEM((2, NY) + slab, BF), pltpu.VMEM((2, NY) + slab, BF),
        pltpu.VMEM((4,) + slab, BF), pltpu.VMEM((2, NY, 2) + slab, BF), pltpu.VMEM((2, NY, 2) + slab, BF),
        pltpu.VMEM((H, ROWS, 2 * S * E), BF),
        pltpu.VMEM((2, H, NX, ROWS // NX, HALF), BF), pltpu.VMEM((2, H, NX - 1, ROWS // NX, HALF), BF),
        pltpu.VMEM((2, H, NZ, SHARE, HALF), BF), pltpu.VMEM((2, H, NZ - 1, SHARE, HALF), BF),
        pltpu.VMEM((2, H, NX, NZ, SHARE, HALF), BF), pltpu.VMEM((H, NZ, SHARE, B), F32), pltpu.VMEM((H, NX, SHARE, B), F32),
        pltpu.VMEM((2, 2, H, S, E, B), BF), pltpu.VMEM((NY, H, S, E, B), BF),
        dma((4,)), dma, dma((S,)), dma, dma,
        dma, dma((2, NY - 1)), dma, dma((2, NY - 1)), dma, dma((2,)), dma, dma((2,)),
        dma, dma((2, H)), dma, dma((2, H)), dma, dma((2, H)), dma, dma((H,)), dma, dma((H,)), dma, dma((H,)), dma, dma,
    ]
    anywhere = pl.BlockSpec(memory_space=pl.ANY)
    vmem = pl.BlockSpec(memory_space=pltpu.VMEM)
    attended = pl.pallas_call(
        kernel,
        out_shape=jax.ShapeDtypeStruct((S, B, D), BF),
        in_specs=[anywhere, vmem, anywhere, anywhere, anywhere],
        out_specs=vmem,
        scratch_shapes=scratch,
        compiler_params=pltpu.CompilerParams(
            collective_id=0, has_side_effects=True, vmem_limit_bytes=56 * 1024 * 1024
        ),
        name="tied_row_attention",
    )(rows, gain, wq, wk, wv)
    mixed = jnp.dot(attended.reshape(S * B, D), wf, preferred_element_type=F32).astype(BF)
    return mixed.reshape(S, B, D)


def solution(mesh):
    placed = (P("seq", "res", None), P(), P(), P(), P(), P())
    return jax.shard_map(
        body, mesh=mesh, in_specs=placed, out_specs=P("seq", "res", None), check_vma=False
    )
```

time: 90.8 us -> 83.7 us (0.922)
  Pallas kernels: 88.1 us -> 81.1 us
    pallas_call x1, Pallas kernels: 88.1 us -> 81.1 us  [body(): pl.pallas_call(kernel, out_shape=jax.ShapeDtypeStruct((S, B, D), BF), in_...]
where the time goes in v3:
time: 83.7 us; the launch traced here: 83.6 us
  Pallas kernels  81.1 us (97%)
  matrix products  2.51 us (3%)
    pallas_call x1, Pallas kernels, body(): pl.pallas_call(kernel, out_shape=jax.ShapeDtypeStruct((S, B, D), BF), in_...  81.1 us
    dot_general x1, matrix products, body(): jnp.dot(attended.reshape(S * B, D), wf, preferred_element_type=F32)  2.51 us

profile of v3, /device:TPU:33, one launch (start us, length us, event | category | flops | bytes accessed | tf_op | source)
XLA Modules:
  0.0 83.6 jit_solution(12834791814863485927)
XLA Ops:
  0.0 0.0 copy-start
  0.0 81.1 %tied_row_attention.1 = bf16[3,128,768]{2,1,0:T(8,128)(2,1)} custom-call(bf16[3,128,768]{2,1,0:T(8,128)(2,1)} %x_hbm.1, f32[768]{0:T(1024)} %gain_ref.1, bf16[768,768]{1,0:T(8,128)(2,1)} %wq_hbm.1, bf16[768,768]{1,0:T(8,128)(2,1)} %wk_hbm.1, bf16[768,768]{1,0:T(8,128)(2,1)} %wv_hbm.1), custom_call_target="tpu_custom_call" | custom-call | tf_op jit(solution)/shard_map/tied_row_attention/pallas_call | solution.py:386
  81.1 0.0 copy-done
  81.1 2.5 %convolution_convert_fusion = bf16[384,768]{1,0:T(8,128)(2,1)} fusion(bf16[384,768]{1,0:T(8,128)(2,1)} %bitcast.4, bf16[768,768]{1,0:T(8,128)(2,1)S(1)} %copy-done), kind=kOutput, calls=%fused_computation | convolution fusion | flops 453279744 | bytes 2359296 | tf_op jit(solution)/shard_map/dot_general | solution.py:397
Async XLA Ops:
  0.0 81.1 %copy-start = (bf16[768,768]{1,0:T(8,128)(2,1)S(1)}, bf16[768,768]{1,0:T(8,128)(2,1)}, u32[]{:S(2)}) copy-start(bf16[768,768]{1,0:T(8,128)(2,1)} %param.11) | copy-start | bytes 3538948

commit v4 on v3

v4 whole, which is shorter than its diff:
```python
import jax
import jax.numpy as jnp
from jax import lax
from jax.experimental import pallas as pl
from jax.experimental.pallas import tpu as pltpu
from jax.sharding import PartitionSpec as P

MESH = pl.DeviceIdType.MESH
BF = jnp.bfloat16
F32 = jnp.float32
NX, NY, NZ = 4, 4, 4
S, B, D = 3, 128, 768
H, E = 3, 64
ROWS = 256
HALF = NY * B
QUARTER = HALF // 2
CHUNKS, CHUNK = 4, B // 4
SHARE = ROWS // NX // NZ


def kernel(
    x_hbm, gain_ref, wq_hbm, wk_hbm, wv_hbm, out_ref,
    xo, xp, xn, wq, wk, wv, wide, qt, kt, vt, kn, qr, kr, vr, kf, qn, qz,
    xs, xr, zs, zr, pf, xsf, xrf, zsf, zrf, pff, fz, ff, os, orr,
    lsem, zss, zrs, qss, qrs, kss, krs, vss, vrs, nss, nrs, kfs, kfr, vfs, vfr, nfs, nfr,
    xss, xrs, lss, lrs, pzs, pzr, pxs, pxr, pnr, fzs, fzr, fxs, fxr, oss, osr,
):
    seq, res = lax.axis_index("seq"), lax.axis_index("res")
    c, x, zl = lax.rem(seq, 2), lax.rem(seq // 2, NX), seq // (2 * NX)
    y, zh = lax.rem(res, NY), res // NY

    def dev(x=x, zl=zl, c=c, y=y, zh=zh):
        return ((zl * NX + x) * 2 + c, zh * NY + y)

    def up(i, d, n):
        return lax.rem(i + d, n)

    other = dev(c=1 - c)

    def send(src, dst, ss, rs, to):
        return pltpu.make_async_remote_copy(
            src_ref=src, dst_ref=dst, send_sem=ss, recv_sem=rs, device_id=to, device_id_type=MESH
        )

    loads = [
        pltpu.make_async_copy(a, b, lsem.at[i])
        for i, (a, b) in enumerate(((x_hbm, xo), (wq_hbm, wq), (wk_hbm, wk), (wv_hbm, wv)))
    ]
    for copy in loads:
        copy.start()

    barrier = pltpu.get_barrier_semaphore()
    peers = [other, dev(zh=1 - zh)]
    peers += [dev(x=up(x, d, NX)) for d in range(1, NX)]
    peers += [dev(zl=up(zl, d, NZ)) for d in range(1, NZ)]
    peers += [dev(y=up(y, d, NY), c=k) for d in range(1, NY) for k in range(2)]
    for peer in peers:
        pl.semaphore_signal(barrier, inc=1, device_id=peer, device_id_type=MESH)
    pl.semaphore_wait(barrier, len(peers))

    loads[0].wait()

    def landed(ref, rs):
        send(ref, ref, rs, rs, other).wait_recv()

    def left(ref, ss):
        send(ref, ref, ss, ss, other).wait_send()

    def rows_over(q):
        rows = pl.ds(q * CHUNK, CHUNK)
        return send(xo.at[:, rows], xp.at[:, rows], zss, zrs.at[q], dev(zh=1 - zh))

    for q in range(CHUNKS):
        rows_over(q).start()

    def norm(rows):
        rows = rows.astype(F32)
        center = rows - jnp.mean(rows, axis=-1, keepdims=True)
        spread = jnp.mean(center * center, axis=-1, keepdims=True)
        return (center * lax.rsqrt(spread + 1e-05) * gain_ref[...].reshape(1, D)).astype(BF)

    def project(normed, w):
        out = jnp.dot(normed, w[...], preferred_element_type=F32).astype(BF)
        return out.T.reshape(NY, H, E, B)

    def q_copy(s, d):
        b = (-d) % NY
        to = dev(y=up(y, d, NY), c=b // 2)
        return send(qt.at[up(y, d, NY), s], qr.at[b % 2 * 2 + c, s], qss, qrs, to)

    def k_copy(s, d):
        g = up(y, d, NY)
        return send(kt.at[g, s], kr.at[(-d) % NY, c, s], kss, krs.at[d - 1], dev(y=g))

    def v_copy(half, s, d):
        g = up(y, d, NY)
        return send(vt.at[half, g, s], vr.at[half, (-d) % NY, c, s], vss, vrs.at[half, d - 1], dev(y=g))

    def far_copy(q, d):
        g = up(y, d, NY)
        return send(kn.at[g, q], kf.at[(-d) % NY, c, q], nss, nrs.at[q // 2, d - 1], dev(y=g))

    def pair(q):
        return pl.ds(2 * q, 2)

    def k_forward(rel):
        part = kr.at[rel, c]
        return send(part, part, kfs, kfr, other)

    def v_forward(half, rel):
        part = vr.at[half, rel, c]
        return send(part, part, vfs, vfr.at[half], other)

    def far_forward(q, rel):
        part = kf.at[rel, c, pair(q)]
        return send(part, part, nfs, nfr.at[q], other)

    for copy in loads[1:3]:
        copy.wait()

    @pl.loop(0, S)
    def _(s):
        normed = norm(xo[s])
        xn[0, s] = normed
        qt[:, s] = project(normed, wq)
        kt[:, s] = project(normed, wk)
        for d in range(1, NY):
            q_copy(s, d).start()

        @pl.when(c == 1)
        def _():
            q_copy(s, 0).start()

        @pl.when(c == 0)
        def _():
            qr[0, s] = qt[y, s]

        for d in range(1, NY):
            k_copy(s, d).start()
        kr[0, c, s] = kt[y, s]

    k_forward(0).start()
    loads[3].wait()

    for g in range(NY):
        wide[:, g * 2 * B : g * 2 * B + H * E] = wk[:, g * H * E : (g + 1) * H * E]
        wide[:, g * 2 * B + H * E : (g + 1) * 2 * B] = jnp.zeros((D, 2 * B - H * E), BF)

    def values(half):
        @pl.loop(0, S)
        def _(s):
            vt[half, :, s] = project(xn[half, s], wv)
            vr[half, 0, c, s] = vt[half, y, s]

        v_forward(half, 0).start()

    values(0)

    def partner(q):
        rows_over(q).wait_recv()
        normed = norm(xp[:, q * CHUNK : (q + 1) * CHUNK].reshape(S * CHUNK, D))
        xn[1, :, q * CHUNK : (q + 1) * CHUNK] = normed.reshape(S, CHUNK, D)
        keys = jnp.dot(normed, wide[...], preferred_element_type=F32).astype(BF).reshape(S, CHUNK, NY * 2 * B)
        for g in range(NY):
            kn[g, q] = keys[:, :, g * 2 * B : (g + 1) * 2 * B]
        for d in range(1, NY):
            far_copy(q, d).start()
        kf[0, c, q] = kn[y, q]

    def columns(r, h):
        return jnp.concatenate([r[rel, :, :, h].reshape(2 * S * E, B) for rel in range(NY)], axis=1)

    def key_rows(part, tile):
        lanes = pl.ds(tile * B, B)
        return jnp.concatenate(
            [
                jnp.concatenate(
                    [kf[rel, i, pair(part), s, :, lanes].reshape(2 * CHUNK, B) for rel in range(NY)], axis=0
                )
                for i in range(2)
                for s in range(S)
            ],
            axis=1,
        )

    def piece(near, far, p):
        return far.at[p - 1] if p else near

    def x_copy(p, h, d):
        g = up(x, d, NX)
        return send(
            piece(xs, xsf, p).at[h, g], piece(xr, xrf, p).at[h, d - 1], xss.at[min(p, 1)], xrs.at[p, h], dev(x=g)
        )

    above, below = up(x, 1, NX), up(x, 3, NX)

    def gather_first(h):
        part = pf.at[h, x]
        return [send(part, part, pxs.at[0], pnr.at[h], dev(x=to)) for to in (above, below)]

    def gather_second(h):
        landed(pf.at[h, pl.ds(0, 2)], pnr.at[h])
        for source, to, first in ((below, above, 0), (above, below, 2)):
            part = pf.at[h, source, pl.ds(first, 2)]
            send(part, part, pxs.at[0], pxr.at[0, h], dev(x=to)).start()

    def z_copy(p, h, d):
        g = up(zl, d, NZ)
        return send(
            piece(zs, zsf, p).at[h, g], piece(zr, zrf, p).at[h, d - 1], lss.at[min(p, 1)], lrs.at[p, h], dev(zl=g)
        )

    def pz_copy(p, h, d):
        part = piece(pf, pff, p).at[h, x, zl]
        return send(part, part, pzs.at[min(p, 1)], pzr.at[p, h], dev(zl=up(zl, d, NZ)))

    def px_copy(p, h, d):
        part = piece(pf, pff, p).at[h, x]
        return send(part, part, pxs.at[min(p, 1)], pxr.at[p, h], dev(x=up(x, d, NX)))

    def fz_copy(d):
        part = fz.at[zl]
        return send(part, part, fzs, fzr, dev(zl=up(zl, d, NZ)))

    def fx_copy(d):
        part = ff.at[x]
        return send(part, part, fxs, fxr, dev(x=up(x, d, NX)))

    def logits(p):
        if p:
            landed(kf.at[:, c, pair(p - 1)], nfr.at[p - 1])
            rows = [key_rows(p - 1, tile) for tile in range(2)]
        else:
            landed(kr.at[:, c], kfr)
        for h in range(H):
            if p:
                part = lax.dot_general(
                    qz[h], rows[h // 2], (((1,), (1,)), ((), ())), preferred_element_type=F32
                ).astype(BF)
                xsf[p - 1, h] = part.reshape(NX, ROWS // NX, QUARTER)
            else:
                part = jnp.dot(qn[h], columns(kr, h), preferred_element_type=F32).astype(BF)
                xs[h] = part.reshape(NX, ROWS // NX, HALF)
            for d in range(1, NX):
                x_copy(p, h, d).start()

    def over_x(p, h):
        mine, theirs, into = piece(xs, xsf, p), piece(xr, xrf, p), piece(zs, zsf, p)
        landed(theirs.at[h], xrs.at[p, h])
        total = mine[h, x].astype(F32)
        for d in range(1, NX):
            total += theirs[h, d - 1].astype(F32)
        into[h] = total.astype(BF).reshape(NZ, SHARE, total.shape[-1])
        for d in range(1, NZ):
            z_copy(p, h, d).start()

    scale = 1.0 / (8.0 * (96.0**0.5))
    tops, sums = [[], []], [[], []]
    lane = lax.broadcasted_iota(jnp.int32, (SHARE, B), 1)
    factors = [jnp.zeros((SHARE, B), F32)]

    def softmax(p, h):
        mine, theirs = piece(zs, zsf, p), piece(zr, zrf, p)
        landed(theirs.at[h], lrs.at[p, h])
        total = mine[h, zl].astype(F32)
        for d in range(1, NZ):
            total += theirs[h, d - 1].astype(F32)
        top = jnp.max(total, axis=-1, keepdims=True)
        if p:
            top = jnp.maximum(top, tops[p - 1][h])
        weights = jnp.exp((total - top) * scale)
        whole = jnp.sum(weights, axis=-1, keepdims=True)
        if p < 2:
            tops[p].append(top)
            sums[p].append(whole)
        else:
            old = [jnp.exp((tops[i][h] - top) * scale) for i in range(2)]
            inverse = 1.0 / (old[0] * sums[0][h] + old[1] * sums[1][h] + whole)
            weights *= inverse
            for i in range(2):
                factors[0] = jnp.where(lane == 4 * i + h, old[i] * inverse, factors[0])
        piece(pf, pff, p)[h, x, zl] = weights.astype(BF)
        for d in range(1, NZ):
            pz_copy(p, h, d).start()

    def pass_on(p, h):
        landed(piece(pf, pff, p).at[h, x, pl.ds(0, NZ - 1)], pzr.at[p, h])
        for copy in [px_copy(p, h, d) for d in range(1, NX)] if p else gather_first(h):
            copy.start()

    def share_keys(part):
        for d in range(1, NY):
            landed(kf.at[(-d) % NY, c, pair(part)], nrs.at[part, d - 1])
            far_forward(part, (-d) % NY).start()

    def share_values(half):
        for d in range(1, NY):
            landed(vr.at[half, (-d) % NY, c], vrs.at[half, d - 1])
            v_forward(half, (-d) % NY).start()

    partner(0)
    for d in range(1, NY):
        landed(kr.at[(-d) % NY, c], krs.at[d - 1])
        k_forward((-d) % NY).start()
    @pl.when(c == 0)
    def _():
        landed(qr.at[pl.ds(1, 3)], qrs)

    @pl.when(c == 1)
    def _():
        landed(qr, qrs)

    @pl.loop(0, H)
    def _(h):
        cols = [qr[2 * b : 2 * b + 2, :, h].reshape(2 * S * E, B).T for b in range(2)]
        qn[h] = jnp.concatenate(cols, axis=0)

    logits(0)
    partner(1)
    far_forward(0, 0).start()
    none = jnp.zeros((E, ROWS), BF)
    for h in range(H):
        rows = []
        for i in range(2):
            for s in range(S):
                query = jnp.concatenate([qr[2 * b + i, s, h] for b in range(2)], axis=1)
                rows += [none, query] if h == 1 else [query, none]
        qz[h] = jnp.concatenate(rows, axis=0).T

    partner(2)
    share_keys(0)
    over_x(0, 0)
    logits(1)
    over_x(0, 1)
    over_x(0, 2)
    partner(3)
    far_forward(1, 0).start()
    values(1)

    @pl.loop(0, 2)
    def _(half):
        @pl.loop(0, S)
        def _(s):
            for d in range(1, NY):
                v_copy(half, s, d).start()

    for h in range(H):
        over_x(1, h)
    share_keys(1)
    for h in range(H):
        softmax(0, h)
    logits(2)
    for h in range(H):
        softmax(1, h)
    over_x(2, 0)
    for h in range(H):
        pass_on(0, h)
    over_x(2, 1)
    over_x(2, 2)
    softmax(2, 0)
    for h in range(H):
        pass_on(1, h)
    softmax(2, 1)
    gather_second(0)
    softmax(2, 2)
    fz[zl] = factors[0]
    for d in range(1, NZ):
        fz_copy(d).start()
    gather_second(1)
    gather_second(2)
    share_values(0)
    share_values(1)
    pass_on(2, 0)
    landed(fz.at[pl.ds(0, NZ - 1)], fzr)
    packed = fz[0]
    for k in range(1, NZ):
        packed = jnp.where((lane >= 8 * k) & (lane < 8 * k + 8), pltpu.roll(fz[k], 8 * k, 1), packed)
    ff[x] = packed
    for d in range(1, NX):
        fx_copy(d).start()
    pass_on(2, 1)
    pass_on(2, 2)
    for half in range(2):
        landed(vr.at[half, :, c], vfr.at[half])

    def o_copy(slot, k, h):
        b = 2 * c + slot
        return send(os.at[slot, k, h], orr.at[y, h], oss, osr, dev(y=up(y, b, NY), c=k))

    landed(ff.at[pl.ds(0, NX - 1)], fxr)
    for h in range(H):
        landed(pf.at[h, 0], pxr.at[0, h])
        for p in (1, 2):
            landed(pff.at[p - 1, h, pl.ds(0, NX - 1)], pxr.at[p, h])
        own = [
            jnp.concatenate(
                [ff[i, :, 8 * k + 4 * n + h : 8 * k + 4 * n + h + 1] for i in range(NX) for k in range(NZ)], axis=0
            )
            for n in range(2)
        ]
        near = (pf[h].reshape(ROWS, HALF).astype(F32) * own[0]).astype(BF)
        first = pff[0, h].reshape(ROWS, QUARTER).astype(F32) * own[1]
        second = pff[1, h].reshape(ROWS, QUARTER).astype(F32)
        low = lax.broadcasted_iota(jnp.int32, (ROWS, B), 1) < B // 2
        far = []
        for k in range(2):
            one, two = first[:, k * B : (k + 1) * B], second[:, k * B : (k + 1) * B]
            far.append(jnp.where(low, one, pltpu.roll(two, B // 2, 1)))
            far.append(jnp.where(low, pltpu.roll(one, B // 2, 1), two))
        far = jnp.concatenate(far, axis=1).astype(BF)
        total = jnp.zeros((2 * S * E, ROWS), F32)
        for half, weights in enumerate((near, far)):
            total += lax.dot_general(
                columns(vr.at[half], h), weights, (((1,), (1,)), ((), ())), preferred_element_type=F32
            )
        total = total.astype(BF)
        for b in range(2):
            os[b, :, h] = total[:, b * B : (b + 1) * B].reshape(2, S, E, B)
        for slot, k in ((1, 0), (1, 1), (0, 1)):
            o_copy(slot, k, h).start()

        @pl.when(c == 1)
        def _():
            o_copy(0, 0, h).start()

        @pl.when(c == 0)
        def _():
            orr[y, h] = os[0, 0, h]

    @pl.when(c == 0)
    def _():
        landed(orr.at[pl.ds(1, 3)], osr)

    @pl.when(c == 1)
    def _():
        landed(orr, osr)

    @pl.loop(0, S)
    def _(s):
        out_ref[s] = orr[:, :, s].reshape(D, B).T

    left(xo, zss)
    left(kt.at[pl.ds(1, NY - 1)], kss)
    left(vt.at[:, pl.ds(1, NY - 1)], vss)
    left(kn.at[pl.ds(1, NY - 1)], nss)
    left(kr.at[:, c], kfs)
    left(vr.at[:, :, c], vfs)
    left(kf.at[:, c], nfs)
    left(xs.at[:, pl.ds(1, NX - 1)], xss.at[0])
    left(xsf.at[:, :, pl.ds(1, NX - 1)], xss.at[1])
    left(zs.at[:, pl.ds(1, NZ - 1)], lss.at[0])
    left(zsf.at[:, :, pl.ds(1, NZ - 1)], lss.at[1])
    left(pf.at[:, 0, pl.ds(1, NZ - 1)], pzs.at[0])
    left(pff.at[:, :, 0, pl.ds(1, NZ - 1)], pzs.at[1])
    left(pf.at[:, pl.ds(1, NX - 1)], pxs.at[0])
    left(pff.at[:, :, pl.ds(1, NX - 1)], pxs.at[1])
    left(fz.at[pl.ds(1, NZ - 1)], fzs)
    left(ff.at[pl.ds(1, NX - 1)], fxs)

    @pl.when(c == 0)
    def _():
        left(qt.at[pl.ds(1, 3)], qss)
        left(orr.at[pl.ds(1, 3)], oss)

    @pl.when(c == 1)
    def _():
        left(qt, qss)
        left(orr, oss)


def body(rows, gain, wq, wk, wv, wf):
    slab = (S, H, E, B)
    dma, vm = pltpu.SemaphoreType.DMA, pltpu.VMEM
    scratch = [
        vm((S, B, D), BF), vm((S, B, D), BF), vm((2, S, B, D), BF),
        vm((D, D), BF), vm((D, D), BF), vm((D, D), BF), vm((D, NY * 2 * B), BF),
        vm((NY,) + slab, BF), vm((NY,) + slab, BF), vm((2, NY) + slab, BF), vm((NY, CHUNKS, S, CHUNK, 2 * B), BF),
        vm((4,) + slab, BF), vm((NY, 2) + slab, BF), vm((2, NY, 2) + slab, BF),
        vm((NY, 2, CHUNKS, S, CHUNK, 2 * B), BF), vm((H, ROWS, 2 * S * E), BF), vm((H, ROWS, 4 * S * E), BF),
        vm((H, NX, ROWS // NX, HALF), BF), vm((H, NX - 1, ROWS // NX, HALF), BF),
        vm((H, NZ, SHARE, HALF), BF), vm((H, NZ - 1, SHARE, HALF), BF), vm((H, NX, NZ, SHARE, HALF), BF),
        vm((2, H, NX, ROWS // NX, QUARTER), BF), vm((2, H, NX - 1, ROWS // NX, QUARTER), BF),
        vm((2, H, NZ, SHARE, QUARTER), BF), vm((2, H, NZ - 1, SHARE, QUARTER), BF),
        vm((2, H, NX, NZ, SHARE, QUARTER), BF),
        vm((NZ, SHARE, B), F32), vm((NX, SHARE, B), F32), vm((2, 2, H, S, E, B), BF), vm((NY, H, S, E, B), BF),
        dma((4,)), dma, dma((CHUNKS,)), dma, dma, dma, dma((NY - 1,)), dma, dma((2, NY - 1)), dma, dma((2, NY - 1)),
        dma, dma, dma, dma((2,)), dma, dma((2,)),
        dma((2,)), dma((3, H)), dma((2,)), dma((3, H)), dma((2,)), dma((3, H)), dma((2,)), dma((3, H)), dma((H,)),
        dma, dma, dma, dma, dma, dma,
    ]
    anywhere = pl.BlockSpec(memory_space=pl.ANY)
    vmem = pl.BlockSpec(memory_space=pltpu.VMEM)
    attended = pl.pallas_call(
        kernel,
        out_shape=jax.ShapeDtypeStruct((S, B, D), BF),
        in_specs=[anywhere, vmem, anywhere, anywhere, anywhere],
        out_specs=vmem,
        scratch_shapes=scratch,
        compiler_params=pltpu.CompilerParams(
            collective_id=0, has_side_effects=True, vmem_limit_bytes=56 * 1024 * 1024
        ),
        name="tied_row_attention",
    )(rows, gain, wq, wk, wv)
    mixed = jnp.dot(attended.reshape(S * B, D), wf, preferred_element_type=F32).astype(BF)
    return mixed.reshape(S, B, D)


def solution(mesh):
    placed = (P("seq", "res", None), P(), P(), P(), P(), P())
    return jax.shard_map(
        body, mesh=mesh, in_specs=placed, out_specs=P("seq", "res", None), check_vma=False
    )
```

time: 83.7 us -> 79.8 us (0.953)
  Pallas kernels: 81.1 us -> 76.6 us
    pallas_call x1, Pallas kernels: 81.1 us -> 76.6 us  [body(): pl.pallas_call(kernel, out_shape=jax.ShapeDtypeStruct((S, B, D), BF), in_...]
where the time goes in v4:
time: 79.8 us; the launch traced here: 79.2 us
  Pallas kernels  76.6 us (96%)
  matrix products  2.51 us (3%)
    pallas_call x1, Pallas kernels, body(): pl.pallas_call(kernel, out_shape=jax.ShapeDtypeStruct((S, B, D), BF), in_...  76.6 us
    dot_general x1, matrix products, body(): jnp.dot(attended.reshape(S * B, D), wf, preferred_element_type=F32)  2.51 us

profile of v4, /device:TPU:33, one launch (start us, length us, event | category | flops | bytes accessed | tf_op | source)
XLA Modules:
  0.0 79.2 jit_solution(291390311863847758)
XLA Ops:
  0.0 0.0 copy-start
  0.0 76.6 %tied_row_attention.1 = bf16[3,128,768]{2,1,0:T(8,128)(2,1)} custom-call(bf16[3,128,768]{2,1,0:T(8,128)(2,1)} %x_hbm.1, f32[768]{0:T(1024)} %gain_ref.1, bf16[768,768]{1,0:T(8,128)(2,1)} %wq_hbm.1, bf16[768,768]{1,0:T(8,128)(2,1)} %wk_hbm.1, bf16[768,768]{1,0:T(8,128)(2,1)} %wv_hbm.1), custom_call_target="tpu_custom_call" | custom-call | tf_op jit(solution)/shard_map/tied_row_attention/pallas_call | solution.py:493
  76.7 0.0 copy-done
  76.7 2.5 %convolution_convert_fusion = bf16[384,768]{1,0:T(8,128)(2,1)} fusion(bf16[384,768]{1,0:T(8,128)(2,1)} %bitcast.4, bf16[768,768]{1,0:T(8,128)(2,1)S(1)} %copy-done), kind=kOutput, calls=%fused_computation | convolution fusion | flops 453279744 | bytes 2359296 | tf_op jit(solution)/shard_map/dot_general | solution.py:504
Async XLA Ops:
  0.0 76.7 %copy-start = (bf16[768,768]{1,0:T(8,128)(2,1)S(1)}, bf16[768,768]{1,0:T(8,128)(2,1)}, u32[]{:S(2)}) copy-start(bf16[768,768]{1,0:T(8,128)(2,1)} %param.11) | copy-start | bytes 3538948

commit v5 on v4

--- a/solution.py
+++ b/solution.py
@@ -19,8 +19,8 @@
 
 
 def kernel(
-    x_hbm, gain_ref, wq_hbm, wk_hbm, wv_hbm, out_ref,
-    xo, xp, xn, wq, wk, wv, wide, qt, kt, vt, kn, qr, kr, vr, kf, qn, qz,
+    x_hbm, gain_hbm, wq_hbm, wk_hbm, wv_hbm, out_ref,
+    xo, gain_ref, xp, xn, wq, wk, wv, wide, qt, kt, vt, kn, qr, kr, vr, kf, qn, qz,
     xs, xr, zs, zr, pf, xsf, xrf, zsf, zrf, pff, fz, ff, os, orr,
     lsem, zss, zrs, qss, qrs, kss, krs, vss, vrs, nss, nrs, kfs, kfr, vfs, vfr, nfs, nfr,
     xss, xrs, lss, lrs, pzs, pzr, pxs, pxr, pnr, fzs, fzr, fxs, fxr, oss, osr,
@@ -42,13 +42,6 @@
             src_ref=src, dst_ref=dst, send_sem=ss, recv_sem=rs, device_id=to, device_id_type=MESH
         )
 
-    loads = [
-        pltpu.make_async_copy(a, b, lsem.at[i])
-        for i, (a, b) in enumerate(((x_hbm, xo), (wq_hbm, wq), (wk_hbm, wk), (wv_hbm, wv)))
-    ]
-    for copy in loads:
-        copy.start()
-
     barrier = pltpu.get_barrier_semaphore()
     peers = [other, dev(zh=1 - zh)]
     peers += [dev(x=up(x, d, NX)) for d in range(1, NX)]
@@ -56,6 +49,13 @@
     peers += [dev(y=up(y, d, NY), c=k) for d in range(1, NY) for k in range(2)]
     for peer in peers:
         pl.semaphore_signal(barrier, inc=1, device_id=peer, device_id_type=MESH)
+    loads = [
+        pltpu.make_async_copy(a, b, lsem.at[i])
+        for i, (a, b) in enumerate(((x_hbm, xo), (gain_hbm, gain_ref), (wq_hbm, wq), (wk_hbm, wk), (wv_hbm, wv)))
+    ]
+    for copy in loads:
+        copy.start()
+
     pl.semaphore_wait(barrier, len(peers))
 
     loads[0].wait()
@@ -115,7 +115,7 @@
         part = kf.at[rel, c, pair(q)]
         return send(part, part, nfs, nfr.at[q], other)
 
-    for copy in loads[1:3]:
+    for copy in loads[1:4]:
         copy.wait()
 
     @pl.loop(0, S)
@@ -140,7 +140,7 @@
         kr[0, c, s] = kt[y, s]
 
     k_forward(0).start()
-    loads[3].wait()
+    loads[4].wait()
 
     for g in range(NY):
         wide[:, g * 2 * B : g * 2 * B + H * E] = wk[:, g * H * E : (g + 1) * H * E]
@@ -298,7 +298,13 @@
             landed(vr.at[half, (-d) % NY, c], vrs.at[half, d - 1])
             v_forward(half, (-d) % NY).start()
 
+    def send_values(half, s):
+        for d in range(1, NY):
+            v_copy(half, s, d).start()
+
     partner(0)
+    for s in range(S):
+        send_values(0, s)
     for d in range(1, NY):
         landed(kr.at[(-d) % NY, c], krs.at[d - 1])
         k_forward((-d) % NY).start()
@@ -336,30 +342,27 @@
     partner(3)
     far_forward(1, 0).start()
     values(1)
-
-    @pl.loop(0, 2)
-    def _(half):
-        @pl.loop(0, S)
-        def _(s):
-            for d in range(1, NY):
-                v_copy(half, s, d).start()
-
-    for h in range(H):
-        over_x(1, h)
+    over_x(1, 0)
+    over_x(1, 1)
+    over_x(1, 2)
     share_keys(1)
-    for h in range(H):
-        softmax(0, h)
+    softmax(0, 0)
+    softmax(0, 1)
+    softmax(0, 2)
     logits(2)
-    for h in range(H):
-        softmax(1, h)
+    for s in range(S):
+        send_values(1, s)
+    softmax(1, 0)
+    softmax(1, 1)
+    softmax(1, 2)
     over_x(2, 0)
-    for h in range(H):
-        pass_on(0, h)
+    pass_on(0, 0)
+    pass_on(0, 1)
+    pass_on(0, 2)
     over_x(2, 1)
     over_x(2, 2)
     softmax(2, 0)
-    for h in range(H):
-        pass_on(1, h)
+    pass_on(1, 0)
     softmax(2, 1)
     gather_second(0)
     softmax(2, 2)
@@ -371,6 +374,7 @@
     share_values(0)
     share_values(1)
     pass_on(2, 0)
+    pass_on(1, 1)
     landed(fz.at[pl.ds(0, NZ - 1)], fzr)
     packed = fz[0]
     for k in range(1, NZ):
@@ -379,6 +383,7 @@
     for d in range(1, NX):
         fx_copy(d).start()
     pass_on(2, 1)
+    pass_on(1, 2)
     pass_on(2, 2)
     for half in range(2):
         landed(vr.at[half, :, c], vfr.at[half])
@@ -389,17 +394,20 @@
 
     landed(ff.at[pl.ds(0, NX - 1)], fxr)
     for h in range(H):
-        landed(pf.at[h, 0], pxr.at[0, h])
-        for p in (1, 2):
-            landed(pff.at[p - 1, h, pl.ds(0, NX - 1)], pxr.at[p, h])
         own = [
             jnp.concatenate(
                 [ff[i, :, 8 * k + 4 * n + h : 8 * k + 4 * n + h + 1] for i in range(NX) for k in range(NZ)], axis=0
             )
             for n in range(2)
         ]
+        landed(pf.at[h, 0], pxr.at[0, h])
         near = (pf[h].reshape(ROWS, HALF).astype(F32) * own[0]).astype(BF)
+        total = lax.dot_general(
+            columns(vr.at[0], h), near, (((1,), (1,)), ((), ())), preferred_element_type=F32
+        )
+        landed(pff.at[0, h, pl.ds(0, NX - 1)], pxr.at[1, h])
         first = pff[0, h].reshape(ROWS, QUARTER).astype(F32) * own[1]
+        landed(pff.at[1, h, pl.ds(0, NX - 1)], pxr.at[2, h])
         second = pff[1, h].reshape(ROWS, QUARTER).astype(F32)
         low = lax.broadcasted_iota(jnp.int32, (ROWS, B), 1) < B // 2
         far = []
@@ -407,12 +415,12 @@
             one, two = first[:, k * B : (k + 1) * B], second[:, k * B : (k + 1) * B]
             far.append(jnp.where(low, one, pltpu.roll(two, B // 2, 1)))
             far.append(jnp.where(low, pltpu.roll(one, B // 2, 1), two))
-        far = jnp.concatenate(far, axis=1).astype(BF)
-        total = jnp.zeros((2 * S * E, ROWS), F32)
-        for half, weights in enumerate((near, far)):
-            total += lax.dot_general(
-                columns(vr.at[half], h), weights, (((1,), (1,)), ((), ())), preferred_element_type=F32
-            )
+        total += lax.dot_general(
+            columns(vr.at[1], h),
+            jnp.concatenate(far, axis=1).astype(BF),
+            (((1,), (1,)), ((), ())),
+            preferred_element_type=F32,
+        )
         total = total.astype(BF)
         for b in range(2):
             os[b, :, h] = total[:, b * B : (b + 1) * B].reshape(2, S, E, B)
@@ -472,7 +480,7 @@
     slab = (S, H, E, B)
     dma, vm = pltpu.SemaphoreType.DMA, pltpu.VMEM
     scratch = [
-        vm((S, B, D), BF), vm((S, B, D), BF), vm((2, S, B, D), BF),
+        vm((S, B, D), BF), vm((D,), F32), vm((S, B, D), BF), vm((2, S, B, D), BF),
         vm((D, D), BF), vm((D, D), BF), vm((D, D), BF), vm((D, NY * 2 * B), BF),
         vm((NY,) + slab, BF), vm((NY,) + slab, BF), vm((2, NY) + slab, BF), vm((NY, CHUNKS, S, CHUNK, 2 * B), BF),
         vm((4,) + slab, BF), vm((NY, 2) + slab, BF), vm((2, NY, 2) + slab, BF),
@@ -483,7 +491,7 @@
         vm((2, H, NZ, SHARE, QUARTER), BF), vm((2, H, NZ - 1, SHARE, QUARTER), BF),
         vm((2, H, NX, NZ, SHARE, QUARTER), BF),
         vm((NZ, SHARE, B), F32), vm((NX, SHARE, B), F32), vm((2, 2, H, S, E, B), BF), vm((NY, H, S, E, B), BF),
-        dma((4,)), dma, dma((CHUNKS,)), dma, dma, dma, dma((NY - 1,)), dma, dma((2, NY - 1)), dma, dma((2, NY - 1)),
+        dma((5,)), dma, dma((CHUNKS,)), dma, dma, dma, dma((NY - 1,)), dma, dma((2, NY - 1)), dma, dma((2, NY - 1)),
         dma, dma, dma, dma((2,)), dma, dma((2,)),
         dma((2,)), dma((3, H)), dma((2,)), dma((3, H)), dma((2,)), dma((3, H)), dma((2,)), dma((3, H)), dma((H,)),
         dma, dma, dma, dma, dma, dma,
@@ -493,7 +501,7 @@
     attended = pl.pallas_call(
         kernel,
         out_shape=jax.ShapeDtypeStruct((S, B, D), BF),
-        in_specs=[anywhere, vmem, anywhere, anywhere, anywhere],
+        in_specs=[anywhere] * 5,
         out_specs=vmem,
         scratch_shapes=scratch,
         compiler_params=pltpu.CompilerParams(

time: 79.8 us -> 78 us (0.977)
  the two profiles are of different devices: /device:TPU:33 before, /device:TPU:1 now
where the time goes in v5:
time: 78 us; the launch traced here: 77.8 us
  Pallas kernels  75.3 us (97%)
  matrix products  2.51 us (3%)
    pallas_call x1, Pallas kernels, body(): pl.pallas_call(kernel, out_shape=jax.ShapeDtypeStruct((S, B, D), BF), in_...  75.3 us
    dot_general x1, matrix products, body(): jnp.dot(attended.reshape(S * B, D), wf, preferred_element_type=F32)  2.51 us

profile of v5, /device:TPU:1, one launch (start us, length us, event | category | flops | bytes accessed | tf_op | source)
XLA Modules:
  0.0 77.8 jit_solution(1225919670910809273)
XLA Ops:
  0.0 0.0 copy-start
  0.0 75.3 %tied_row_attention.1 = bf16[3,128,768]{2,1,0:T(8,128)(2,1)} custom-call(bf16[3,128,768]{2,1,0:T(8,128)(2,1)} %x_hbm.1, f32[768]{0:T(1024)} %gain_hbm.1, bf16[768,768]{1,0:T(8,128)(2,1)} %wq_hbm.1, bf16[768,768]{1,0:T(8,128)(2,1)} %wk_hbm.1, bf16[768,768]{1,0:T(8,128)(2,1)} %wv_hbm.1), custom_call_target="tpu_custom_call" | custom-call | tf_op jit(solution)/shard_map/tied_row_attention/pallas_call | solution.py:501
  75.3 0.0 copy-done
  75.3 2.5 %convolution_convert_fusion = bf16[384,768]{1,0:T(8,128)(2,1)} fusion(bf16[384,768]{1,0:T(8,128)(2,1)} %bitcast.4, bf16[768,768]{1,0:T(8,128)(2,1)S(1)} %copy-done), kind=kOutput, calls=%fused_computation | convolution fusion | flops 453279744 | bytes 2359296 | tf_op jit(solution)/shard_map/dot_general | solution.py:512
Async XLA Ops:
  0.0 75.3 %copy-start = (bf16[768,768]{1,0:T(8,128)(2,1)S(1)}, bf16[768,768]{1,0:T(8,128)(2,1)}, u32[]{:S(2)}) copy-start(bf16[768,768]{1,0:T(8,128)(2,1)} %param.11) | copy-start | bytes 3538948

commit v6 on v5

--- a/solution.py
+++ b/solution.py
@@ -505,7 +505,7 @@
         out_specs=vmem,
         scratch_shapes=scratch,
         compiler_params=pltpu.CompilerParams(
-            collective_id=0, has_side_effects=True, vmem_limit_bytes=56 * 1024 * 1024
+            collective_id=0, has_side_effects=True, vmem_limit_bytes=53 * 1024 * 1024
         ),
         name="tied_row_attention",
     )(rows, gain, wq, wk, wv)

time: 78 us -> 76.8 us (0.985)
  matrix products: 2.51 us -> 1.45 us
  Pallas kernels: 75.3 us -> 74.5 us
  local copies, waits for them, and re-layouts: 0.01 us -> 0.79 us
    dot_general x1, matrix products: 2.51 us -> 1.45 us  [body(): jnp.dot(attended.reshape(S * B, D), wf, preferred_element_type=F32)]
    pallas_call x1, Pallas kernels: 75.3 us -> 74.5 us  [body(): pl.pallas_call(kernel, out_shape=jax.ShapeDtypeStruct((S, B, D), BF), in_...]
    unnamed x2 -> x4, local copies, waits for them, and re-layouts: 0.01 us -> 0.79 us
where the time goes in v6:
time: 76.8 us; the launch traced here: 76.7 us
  Pallas kernels  74.5 us (97%)
  matrix products  1.45 us (2%)
  local copies, waits for them, and re-layouts  0.79 us (1%)
    pallas_call x1, Pallas kernels, body(): pl.pallas_call(kernel, out_shape=jax.ShapeDtypeStruct((S, B, D), BF), in_...  74.5 us

profile of v6, /device:TPU:1, one launch (start us, length us, event | category | flops | bytes accessed | tf_op | source)
XLA Modules:
  0.0 76.7 jit_solution(3216655959026671720)
XLA Ops:
  0.0 0.0 copy-start
  0.0 0.0 copy-start.1
  0.0 0.8 %copy-done.1 = f32[768]{0:T(1024)S(1)} copy-done((f32[768]{0:T(1024)S(1)}, f32[768]{0:T(1024)}, u32[]{:S(2)}) %copy-start.1) | copy-done | bytes 3096
  0.8 74.5 %tied_row_attention.1 = bf16[3,128,768]{2,1,0:T(8,128)(2,1)S(1)} custom-call(bf16[3,128,768]{2,1,0:T(8,128)(2,1)} %x_hbm.1, f32[768]{0:T(1024)S(1)} %copy-done.1, bf16[768,768]{1,0:T(8,128)(2,1)} %wq_hbm.1, bf16[768,768]{1,0:T(8,128)(2,1)} %wk_hbm.1, bf16[768,768]{1,0:T(8,128)(2,1)} %wv_hbm.1), custom_call_target="tpu_custom_call" | custom-call | tf_op jit(solution)/shard_map/tied_row_attention/pallas_call | solution.py:501
  75.3 0.0 copy-done
  75.3 1.4 %convolution_convert_fusion = bf16[384,768]{1,0:T(8,128)(2,1)} fusion(bf16[384,768]{1,0:T(8,128)(2,1)S(1)} %bitcast.4, bf16[768,768]{1,0:T(8,128)(2,1)S(1)} %copy-done), kind=kOutput, calls=%fused_computation | convolution fusion | flops 453279744 | bytes 2359296 | tf_op jit(solution)/shard_map/dot_general | solution.py:512
Async XLA Ops:
  0.0 75.3 %copy-start = (bf16[768,768]{1,0:T(8,128)(2,1)S(1)}, bf16[768,768]{1,0:T(8,128)(2,1)}, u32[]{:S(2)}) copy-start(bf16[768,768]{1,0:T(8,128)(2,1)} %param.11) | copy-start | bytes 3538948
  0.0 0.8 %copy-start.1 = (f32[768]{0:T(1024)S(1)}, f32[768]{0:T(1024)}, u32[]{:S(2)}) copy-start(f32[768]{0:T(1024)} %gain_hbm.1) | copy-start | bytes 9220
